TPU v7x, 768 devices: a whole 4x8x12 slice. The times are simulated.
768 devices in a mesh: blk: 192 (over x, y_lo, z), band: 4 (over y_hi, core).
Axes of the slice: x: 4, y: 8 (y_hi: 2, y_lo: 4; y = y_hi * 4 + y_lo), z: 12, core: 2. Of those that a mesh axis runs over, the one named last changes fastest.
Arguments:
- disp_fwd: float32 [192, 4, 25, 2048], P('blk', 'band'), may hold values from -6 to 6
- prev_fwd: float32 [192, 4, 25, 2048], P('blk', 'band'), may hold values from -6 to 6
- disp_adj: float32 [192, 4, 25, 2048], P('blk', 'band'), may hold values from -6 to 6
- prev_adj: float32 [192, 4, 25, 2048], P('blk', 'band'), may hold values from -6 to 6
- modulus: float32 [192, 4, 25, 2048], P('blk', 'band'), may hold values from 0.5 to 2
- radius: float32 [192, 4, 25], P('blk', 'band'), may hold values from 256 to 2048
- step_scale: float32 [192, 4, 25], P('blk', 'band'), may hold values from 0.01 to 0.04
- kernel_in: float32 [192, 4, 25, 2048], P('blk', 'band'), may hold values from -6 to 6
- buckets: int32 [192, 4], P('blk', 'band'), may hold values from 0 to 3
- halo_count: int32 [192, 4, 4], P('blk', 'band'), may hold values from 0 to 8, as said below
- blk_nodes: int32 [192, 4, 2, 8], P('blk', 'band'), may hold values from 0 to 24, as said below
- band_nodes: int32 [192, 4, 2, 4], P('blk', 'band'), may hold values from 0 to 24, as said below
Outputs:
- next_fwd: float32 [192, 4, 25, 2048], P('blk', 'band')
- next_adj: float32 [192, 4, 25, 2048], P('blk', 'band')
- kernel_out: float32 [192, 4, 25, 2048], P('blk', 'band')
Inputs may be any that keep to these rules, and one draw needn't show every extreme that they name: `halo_count`: entries 0 and 1 count the nodes shared with the blk neighbour below and above, entries 2 and 3 with the band neighbour below and above. A device's count toward a neighbour equals the neighbour's count back; counts toward the outside of the grid are zero; some pair along blk shares 8 nodes and some pair along band 4. Slot k of a device's list toward a blk neighbour and slot k of that neighbour's list back hold copies of one node; slots at or past the count are unused. The 24 ids of one device over blk_nodes and band_nodes are all different. `band_nodes`: slot k of a device's list toward a band neighbour and slot k of that neighbour's list back hold copies of one node; slots at or past the count are unused; ids are different from those of blk_nodes on the same device.
All inputs are finite; a program needn't handle non-finite values.
Results may differ from a plain program's by a relative error of at most 0.0046.
Values sent between devices are 32-bit elements; how exact they have to be, the bound alone decides.
No kernel may reach another device: no remote copies, remote signals or barrier semaphores. Data moves between devices by JAX's collectives and lax.ppermute only.
A program may use at most 32 MiB of HBM per device.

v0:
```python
from functools import partial
import math

import jax
import jax.numpy as jnp
import numpy as np
from jax import lax
from jax.sharding import PartitionSpec as P


def shifted(value, axis, steps):
    count = lax.axis_size(axis)
    initial, last = (max(0, -steps), min(count, count - steps))
    return lax.ppermute(value, axis, [(source, source + steps) for source in range(initial, last)])


def gll_tables():
    inner_root = math.sqrt(3.0 / 7.0)
    points = np.array([-1.0, -inner_root, 0.0, inner_root, 1.0])
    weights = np.array([0.1, 49.0 / 90.0, 32.0 / 45.0, 49.0 / 90.0, 0.1])
    legendre = (35.0 * points**4 - 30.0 * points**2 + 3.0) / 8.0
    derivative = np.zeros((5, 5))
    for target in range(5):
        for source in range(5):
            if target != source:
                derivative[target, source] = (
                    legendre[target] / legendre[source] / (points[target] - points[source])
                )
    derivative[0, 0] = -5.0
    derivative[4, 4] = 5.0
    return (
        jnp.asarray(derivative, jnp.float32),
        jnp.asarray(np.outer(weights, weights), jnp.float32),
    )


def azimuth_table(mode_total):
    sample_len = 2 * mode_total
    table_shape = (2 * mode_total, sample_len)
    row_ids = lax.broadcasted_iota(jnp.int32, table_shape, 0)
    col_ids = lax.broadcasted_iota(jnp.int32, table_shape, 1)
    quarter = (row_ids >= mode_total).astype(jnp.int32) * (sample_len // 4)
    phase = (row_ids % mode_total * col_ids + quarter) % sample_len
    factor = math.sqrt(2.0 / sample_len)
    return (jnp.cos(phase.astype(jnp.float32) * (2.0 * math.pi / sample_len)) * factor).astype(
        jnp.bfloat16
    )


def mode_tops(mode_total):
    return [max(mode_total // 64, 1), max(mode_total // 16, 1), max(mode_total // 4, 1), mode_total]


def mode_mask(buckets, mode_total):
    order_tops = mode_tops(mode_total)
    order_limit = jnp.where(
        buckets == 0,
        order_tops[0],
        jnp.where(
            buckets == 1, order_tops[1], jnp.where(buckets == 2, order_tops[2], order_tops[3])
        ),
    )
    kept = (jnp.arange(mode_total, dtype=jnp.int32) < order_limit[..., None]).astype(jnp.float32)
    return jnp.concatenate([kept, kept], axis=-1)


def spin(coeffs, inv_radius, mode_orders):
    half_len = mode_orders.shape[0]
    return (
        jnp.concatenate(
            [-mode_orders * coeffs[..., half_len:], mode_orders * coeffs[..., :half_len]], axis=-1
        )
        * inv_radius
    )


def unspin(coeffs, inv_radius, mode_orders):
    half_len = mode_orders.shape[0]
    return (
        jnp.concatenate(
            [mode_orders * coeffs[..., half_len:], -mode_orders * coeffs[..., :half_len]], axis=-1
        )
        * inv_radius
    )


def to_samples(rows_in, azim_table, top_mode):
    half_len = azim_table.shape[0] // 2
    if top_mode == half_len:
        return jnp.dot(rows_in, azim_table, preferred_element_type=jnp.float32)
    picked = jnp.concatenate(
        [rows_in[:, :top_mode], rows_in[:, half_len : half_len + top_mode]], axis=1
    )
    sub_table = jnp.concatenate(
        [azim_table[:top_mode], azim_table[half_len : half_len + top_mode]], axis=0
    )
    return jnp.dot(picked, sub_table, preferred_element_type=jnp.float32)


def to_modes(rows_in, azim_table, top_mode):
    half_len = azim_table.shape[0] // 2
    contract_dims = (((1,), (1,)), ((), ()))
    if top_mode == half_len:
        return lax.dot_general(
            rows_in, azim_table, contract_dims, preferred_element_type=jnp.float32
        )
    sub_table = jnp.concatenate(
        [azim_table[:top_mode], azim_table[half_len : half_len + top_mode]], axis=0
    )
    result = lax.dot_general(rows_in, sub_table, contract_dims, preferred_element_type=jnp.float32)
    filler = jnp.zeros((rows_in.shape[0], half_len - top_mode), jnp.float32)
    return jnp.concatenate([result[:, :top_mode], filler, result[:, top_mode:], filler], axis=1)


def per_device(
    disp_fwd,
    prev_fwd,
    disp_adj,
    prev_adj,
    modulus,
    radius,
    step_scale,
    kernel_in,
    buckets,
    halo_count,
    blk_nodes,
    band_nodes,
):
    derivative, quadrature = gll_tables()
    element_total = disp_fwd.shape[1]
    coeff_len = disp_fwd.shape[-1]
    mode_total = coeff_len // 2
    sample_len = modulus.shape[-1]
    azim_table = azimuth_table(mode_total)
    mode_orders = jnp.arange(mode_total, dtype=jnp.float32)
    kept_modes = mode_mask(buckets, mode_total)[:, :, None, :]
    inv_radius = 1.0 / radius[..., None]
    field_fwd = disp_fwd * kept_modes
    field_adj = disp_adj * kept_modes
    stacked = jnp.stack(
        [
            field_fwd,
            spin(field_fwd, inv_radius, mode_orders),
            field_adj,
            spin(field_adj, inv_radius, mode_orders),
        ]
    ).astype(jnp.bfloat16)
    rows_in = stacked.reshape(-1, coeff_len)
    order_tops = mode_tops(mode_total)
    highest = jnp.max(buckets)
    samples = lax.switch(
        highest,
        [partial(to_samples, top_mode=level_top) for level_top in order_tops],
        rows_in,
        azim_table,
    )
    samples = samples.reshape(4, element_total, 5, 5, sample_len)
    physical = samples[0::2]
    azimuthal = samples[1::2]
    weight = (modulus.reshape(element_total, 5, 5, sample_len) * quadrature[None, :, :, None])[None]
    grad_s = jnp.einsum("ab,febjk->feajk", derivative, physical, precision=lax.Precision.HIGHEST)
    grad_z = jnp.einsum("ab,feibk->feiak", derivative, physical, precision=lax.Precision.HIGHEST)
    diverge = jnp.einsum(
        "ba,febjk->feajk", derivative, weight * grad_s, precision=lax.Precision.HIGHEST
    ) + jnp.einsum("ba,feibk->feiak", derivative, weight * grad_z, precision=lax.Precision.HIGHEST)
    stress_phi = weight * azimuthal
    back_rows = (
        jnp.stack([diverge[0], stress_phi[0], diverge[1], stress_phi[1]])
        .astype(jnp.bfloat16)
        .reshape(-1, sample_len)
    )
    highest_back = jnp.max(buckets)
    back = lax.switch(
        highest_back,
        [partial(to_modes, top_mode=level_top) for level_top in order_tops],
        back_rows,
        azim_table,
    )
    back = back.reshape(4, 1, element_total, 25, coeff_len)
    stiff_fwd = kept_modes * (back[0] + unspin(back[1], inv_radius, mode_orders))
    stiff_adj = kept_modes * (back[2] + unspin(back[3], inv_radius, mode_orders))
    products = grad_s[0] * grad_s[1] + grad_z[0] * grad_z[1] + azimuthal[0] * azimuthal[1]
    kernel_out = kernel_in - (quadrature[None, :, :, None] * products).reshape(kernel_in.shape)
    stiff_pair = jnp.stack([stiff_fwd, stiff_adj]).reshape(2, element_total * 25, coeff_len)
    blk_lists = blk_nodes[0, 0]
    band_lists = band_nodes[0, 0]
    counts = halo_count[0, 0]
    blk_slots = jnp.arange(blk_lists.shape[1], dtype=jnp.int32)
    band_slots = jnp.arange(band_lists.shape[1], dtype=jnp.int32)
    blk_lower_send = stiff_pair[:, blk_lists[0]]
    blk_upper_send = stiff_pair[:, blk_lists[1]]
    from_below = shifted(blk_upper_send, "blk", 1)
    from_above = shifted(blk_lower_send, "blk", -1)
    band_below = shifted(stiff_pair[:, band_lists[1]], "band", 1)
    band_above = shifted(stiff_pair[:, band_lists[0]], "band", -1)
    total = stiff_pair
    total = total.at[:, blk_lists[0]].add(
        from_below * (blk_slots < counts[0]).astype(jnp.float32)[None, :, None]
    )
    total = total.at[:, blk_lists[1]].add(
        from_above * (blk_slots < counts[1]).astype(jnp.float32)[None, :, None]
    )
    total = total.at[:, band_lists[0]].add(
        band_below * (band_slots < counts[2]).astype(jnp.float32)[None, :, None]
    )
    total = total.at[:, band_lists[1]].add(
        band_above * (band_slots < counts[3]).astype(jnp.float32)[None, :, None]
    )
    total = total.reshape(2, 1, element_total, 25, coeff_len)
    growth = step_scale[..., None]
    next_fwd = kept_modes * (2.0 * field_fwd - prev_fwd - growth * total[0])
    next_adj = kept_modes * (2.0 * field_adj - prev_adj - growth * total[1])
    return (next_fwd, next_adj, kernel_out)


def solution(mesh):
    in_specs = (
        P("blk", "band", None, None),
        P("blk", "band", None, None),
        P("blk", "band", None, None),
        P("blk", "band", None, None),
        P("blk", "band", None, None),
        P("blk", "band", None),
        P("blk", "band", None),
        P("blk", "band", None, None),
        P("blk", "band"),
        P("blk", "band", None),
        P("blk", "band", None, None),
        P("blk", "band", None, None),
    )
    out_specs = (
        P("blk", "band", None, None),
        P("blk", "band", None, None),
        P("blk", "band", None, None),
    )
    return jax.shard_map(
        per_device, mesh=mesh, in_specs=in_specs, out_specs=out_specs, check_vma=False
    )
```

profile of v0, /device:TPU:58, one launch (start us, length us, event | category | flops | bytes accessed | tf_op | source)
XLA Modules:
  0.0 135.5 jit_solution(3012021127464641919)
XLA Ops:
  1.4 0.7 divide_bitcast_fusion
  2.0 1.2 convert_bitcast_fusion.1
  3.6 67.6 %fusion.45 = bf16[2048,2048]{1,0:T(8,128)(2,1)} fusion(s32[2048]{0:T(1024)S(1)} %fusion.80, s32[2048]{0:T(1024)S(1)} %iota_and_fusion, s32[2048]{0:T(1024)S(1)} %fusion.76, pred[2048]{0:T(1024)(128)(4,1)S(1)} %fusion.79), kind=kLoop, calls=%fused_computation.57 | loop fusion | flops 75497472 | bytes 8415232 | tf_op jit(solution)/shard_map/convert_element_type | solution.py:45
  71.2 4.8 %conditional.2 = (f32[100,2048]{1,0:T(8,128)S(1)}) conditional(s32[]{:T(128)} %bitcast.6, (bf16[100,2048]{1,0:T(8,128)(2,1)S(1)}, bf16[2048,2048]{1,0:T(8,128)(2,1)}, bf16[2048,2048]{1,0:T(8,128)(2,1)}) %tuple.32, (bf16[100,2048]{1,0:T(8,128)(2,1)S(1)}, bf16[2048,2048]{1,0:T(8,128)(2,1)}, ...), branch_computations={%region_0.1_spmd, %region_1.2_spmd, %region_2.3_spmd, %region_3.4_... | conditional | flops 838860800 | bytes 9617416 | solution.py:151
  71.2 4.8 %fusion.98 = f32[100,2048]{1,0:T(8,128)S(1)} fusion(bf16[100,2048]{1,0:T(8,128)(2,1)S(1)} %get-tuple-element.54, bf16[2048,2048]{1,0:T(8,128)(2,1)} %get-tuple-element.55), kind=kOutput, calls=%fused_computation.170 | convolution fusion | flops 838860800 | bytes 9617408 | tf_op jit(solution)/shard_map/cond/branch_3_fun/dot_general | solution.py:90
  76.2 0.7 fusion.48
  77.5 0.9 convolution_bitcast_fusion.3
  78.5 1.4 %fusion.93 = (f32[2,1,5,5,2048]{4,2,3,0,1:T(8,128)}, bf16[2,1,5,5,2048]{4,2,3,0,1:T(8,128)(2,1)S(1)}, f32[2,5,5,2048]{3,1,2,0:T(8,128)S(1)}) fusion(f32[2,1,5,5,2048]{4,3,2,0,1:T(8,128)S(1)} %get-tuple-element.98, f32[5,5,2048]{2,0,1:T(8,128)S(1)} %copy_multiply_fusion, f32[2,5,2048,5]{2,3,1,0:T(8,128)S(1)} %fusion.48), kind=kLoop, calls=%fused_computation.165 | loop fusion | flops 307200 | bytes 2048000
  80.0 0.9 fusion.51
  80.9 0.9 fusion.47
  82.5 6.3 %conditional.3 = (f32[100,2048]{1,0:T(8,128)S(1)}) conditional(s32[]{:T(128)} %bitcast.6, (bf16[2048,2048]{1,0:T(8,128)(2,1)}, bf16[2048,2048]{1,0:T(8,128)(2,1)}, bf16[100,2048]{1,0:T(8,128)(2,1)S(1)}) %tuple.34, (bf16[2048,2048]{1,0:T(8,128)(2,1)}, bf16[2048,2048]{1,0:T(8,128)(2,1)}, ...), branch_computations={%region_4.5_spmd, %region_5.6_spmd, %region_6.7_spmd, %region_7.8_... | conditional | flops 838860800 | bytes 9617416 | solution.py:173
  82.7 6.1 %fusion.99 = f32[100,2048]{1,0:T(8,128)S(1)} fusion(bf16[100,2048]{1,0:T(8,128)(2,1)S(1)} %get-tuple-element.68, bf16[2048,2048]{1,0:T(8,128)(2,1)} %get-tuple-element.69), kind=kOutput, calls=%fused_computation.171 | convolution fusion | flops 838860800 | bytes 9617408 | tf_op jit(solution)/shard_map/cond/branch_3_fun/dot_general | solution.py:104
  90.0 0.7 gather_fusion
  90.7 4.3 %collective-permute-start = (f32[2,8,2048]{2,0,1:T(2,128)S(1)}, f32[2,8,2048]{2,0,1:T(2,128)}, u32[]{:S(2)}, u32[]{:S(2)}) collective-permute-start(f32[2,8,2048]{2,0,1:T(2,128)S(1)} %bitcast.144), channel_id=1, source_target_pairs={{0,4},{4,8},{8,12},{12,16},{16,20},{20,24},{24,28},{28,32},{32,36}... | collective-permute-start | bytes 393224 | tf_op jit(solution)/shard_map/ppermute | solution.py:14
  95.0 0.7 gather_fusion.1
  95.6 13.0 %collective-permute-start.1 = (f32[2,8,2048]{2,0,1:T(2,128)S(1)}, f32[2,8,2048]{2,0,1:T(2,128)S(1)}, u32[]{:S(2)}, u32[]{:S(2)}) collective-permute-start(f32[2,8,2048]{2,0,1:T(2,128)S(1)} %bitcast.143), channel_id=1, source_target_pairs={{4,0},{8,4},{12,8},{16,12},{20,16},{24,20},{28,24},{32,28},{36,32}... | collective-permute-start | bytes 393224 | tf_op jit(solution)/shard_map/ppermute | solution.py:14
  109.3 1.9 %collective-permute-start.2 = (f32[2,4,2048]{2,0,1:T(2,128)S(1)}, f32[2,4,2048]{2,0,1:T(2,128)}, u32[]{:S(2)}, u32[]{:S(2)}) collective-permute-start(f32[2,4,2048]{2,0,1:T(2,128)S(1)} %bitcast.148), channel_id=1, source_target_pairs={{0,1},{1,2},{2,3},{4,5},{5,6},{6,7},{8,9},{9,10},{10,11},{12,13},{... | collective-permute-start | bytes 196616 | tf_op jit(solution)/shard_map/ppermute | solution.py:14
  111.3 1.2 gather_fusion.3
  112.5 7.5 %collective-permute-start.3 = (f32[2,4,2048]{2,0,1:T(2,128)}, f32[2,4,2048]{2,0,1:T(2,128)S(1)}, u32[]{:S(2)}, u32[]{:S(2)}) collective-permute-start(f32[2,4,2048]{2,0,1:T(2,128)} %bitcast.55), channel_id=1, source_target_pairs={{1,0},{2,1},{3,2},{5,4},{6,5},{7,6},{9,8},{10,9},{11,10},{13,12},{... | collective-permute-start | bytes 196616 | tf_op jit(solution)/shard_map/ppermute | solution.py:14
  120.3 1.2 fusion.54
  123.0 0.7 compare_convert_fusion.2
  124.2 1.6 %multiply_subtract_fusion = f32[1,1,25,2048]{3,1,2,0:T(1,128)} fusion(f32[1,1,25,2048]{3,1,2,0:T(1,128)S(1)} %copy-done.3, f32[1,1,25,2048]{3,1,2,0:T(1,128)S(1)} %bitcast.142, f32[25]{0:T(128)} %constant.91), kind=kLoop, calls=%fused_computation.107 | loop fusion | flops 102400 | bytes 614500 | tf_op jit(solution)/shard_map/sub | solution.py:183
  125.8 0.6 compare_convert_fusion
  126.5 0.9 multiply_bitcast_fusion.4
  127.6 1.0 multiply_bitcast_fusion.2
  128.6 1.0 scatter_fusion
  129.7 1.0 scatter_fusion.1
  130.7 0.7 scatter_fusion.2
  131.4 0.7 scatter_fusion.3
  132.5 1.2 fusion.64
  133.7 0.9 copy.78
  134.6 0.9 copy.79
  (66 shorter events, 6.5 us)
Async XLA Ops:
  71.2 5.1 %copy-start.6 = (f32[5,5,1,1]{1,0,3,2:T(8,128)S(1)}, f32[5,5,1,1]{1,0,3,2:T(8,128)}, u32[]{:S(2)}) copy-start(f32[5,5,1,1]{1,0,3,2:T(8,128)} %constant.92) | copy-start | bytes 304
  71.2 5.8 %copy-start.2 = (f32[1,1,25,2048]{3,1,2,0:T(1,128)S(1)}, f32[1,1,25,2048]{3,1,2,0:T(1,128)}, u32[]{:S(2)}) copy-start(f32[1,1,25,2048]{3,1,2,0:T(1,128)} %param.26) | copy-start | bytes 614404
  76.0 2.4 %copy-start.8 = (f32[5,5]{0,1:T(8,128)S(1)}, f32[5,5]{0,1:T(8,128)}, u32[]{:S(2)}) copy-start(f32[5,5]{0,1:T(8,128)} %constant.78.clone) | copy-start | bytes 304
  82.5 7.0 %copy-start.9 = (s32[1,1,2,8]{3,2,1,0:T(2,128)S(1)}, s32[1,1,2,8]{3,2,1,0:T(2,128)}, u32[]{:S(2)}) copy-start(s32[1,1,2,8]{3,2,1,0:T(2,128)} %param.32) | copy-start | bytes 196
  82.5 26.1 %copy-start.10 = (s32[1,1,2,4]{3,2,1,0:T(2,128)S(1)}, s32[1,1,2,4]{3,2,1,0:T(2,128)}, u32[]{:S(2)}) copy-start(s32[1,1,2,4]{3,2,1,0:T(2,128)} %param.33) | copy-start | bytes 100
  88.9 32.9 %copy-start.7 = (s32[1,1,4]{2,1,0:T(1,128)S(1)}, s32[1,1,4]{2,1,0:T(1,128)}, u32[]{:S(2)}) copy-start(s32[1,1,4]{2,1,0:T(1,128)} %param.31) | copy-start | bytes 52
  88.9 35.4 %copy-start.3 = (f32[1,1,25,2048]{3,1,2,0:T(1,128)S(1)}, f32[1,1,25,2048]{3,1,2,0:T(1,128)}, u32[]{:S(2)}) copy-start(f32[1,1,25,2048]{3,1,2,0:T(1,128)} %param.29) | copy-start | bytes 614404
  88.9 43.6 %copy-start = (f32[1,1,25,2048]{3,1,2,0:T(1,128)S(1)}, f32[1,1,25,2048]{3,1,2,0:T(1,128)}, u32[]{:S(2)}) copy-start(f32[1,1,25,2048]{3,1,2,0:T(1,128)} %param.22) | copy-start | bytes 614404
  88.9 43.6 %copy-start.1 = (f32[1,1,25,2048]{3,1,2,0:T(1,128)S(1)}, f32[1,1,25,2048]{3,1,2,0:T(1,128)}, u32[]{:S(2)}) copy-start(f32[1,1,25,2048]{3,1,2,0:T(1,128)} %param.24) | copy-start | bytes 614404
  88.9 43.6 %copy-start.4 = (f32[1,1,25,2048]{3,1,2,0:T(1,128)S(1)}, f32[1,1,25,2048]{3,1,2,0:T(1,128)}, u32[]{:S(2)}) copy-start(f32[1,1,25,2048]{3,1,2,0:T(1,128)} %param.25) | copy-start | bytes 614404
  88.9 43.6 %copy-start.5 = (f32[1,1,25,2048]{3,1,2,0:T(1,128)S(1)}, f32[1,1,25,2048]{3,1,2,0:T(1,128)}, u32[]{:S(2)}) copy-start(f32[1,1,25,2048]{3,1,2,0:T(1,128)} %param.23) | copy-start | bytes 614404
  90.7 36.9 %collective-permute-start = (f32[2,8,2048]{2,0,1:T(2,128)S(1)}, f32[2,8,2048]{2,0,1:T(2,128)}, u32[]{:S(2)}, u32[]{:S(2)}) collective-permute-start(f32[2,8,2048]{2,0,1:T(2,128)S(1)} %bitcast.144), channel_id=1, source_target_pairs={{0,4},{4,8},{8,12},{12,16},{16,20},{20,24},{24,28},{28,32},{32,36}... | collective-permute-start | bytes 393224 | tf_op jit(solution)/shard_map/ppermute | solution.py:14
  95.6 33.9 %collective-permute-start.1 = (f32[2,8,2048]{2,0,1:T(2,128)S(1)}, f32[2,8,2048]{2,0,1:T(2,128)S(1)}, u32[]{:S(2)}, u32[]{:S(2)}) collective-permute-start(f32[2,8,2048]{2,0,1:T(2,128)S(1)} %bitcast.143), channel_id=1, source_target_pairs={{4,0},{8,4},{12,8},{16,12},{20,16},{24,20},{28,24},{32,28},{36,32}... | collective-permute-start | bytes 393224 | tf_op jit(solution)/shard_map/ppermute | solution.py:14
  109.3 17.2 %collective-permute-start.2 = (f32[2,4,2048]{2,0,1:T(2,128)S(1)}, f32[2,4,2048]{2,0,1:T(2,128)}, u32[]{:S(2)}, u32[]{:S(2)}) collective-permute-start(f32[2,4,2048]{2,0,1:T(2,128)S(1)} %bitcast.148), channel_id=1, source_target_pairs={{0,1},{1,2},{2,3},{4,5},{5,6},{6,7},{8,9},{9,10},{10,11},{12,13},{... | collective-permute-start | bytes 196616 | tf_op jit(solution)/shard_map/ppermute | solution.py:14
  112.5 15.0 %collective-permute-start.3 = (f32[2,4,2048]{2,0,1:T(2,128)}, f32[2,4,2048]{2,0,1:T(2,128)S(1)}, u32[]{:S(2)}, u32[]{:S(2)}) collective-permute-start(f32[2,4,2048]{2,0,1:T(2,128)} %bitcast.55), channel_id=1, source_target_pairs={{1,0},{2,1},{3,2},{5,4},{6,5},{7,6},{9,8},{10,9},{11,10},{13,12},{... | collective-permute-start | bytes 196616 | tf_op jit(solution)/shard_map/ppermute | solution.py:14
where the time goes:
time: 137 us; the launch traced here: 135 us
  other arithmetic  84.5 us (62%)
  starting transfers between devices  26.8 us (20%)
  matrix products  14.3 us (10%)
  local copies, waits for them, and re-layouts  7.8 us (6%)
  between operations  1.91 us (1%)
    convert_element_type x1, other arithmetic, azimuth_table(): (jnp.cos(phase.astype(jnp.float32) * (2.0 * math.pi / sample_len)) * fact...  67.6 us
    ppermute x4, starting transfers between devices, shifted(): lax.ppermute(value, axis, [(source, source + steps) for source in range(i...  26.8 us
    dot_general x1, matrix products, to_modes(): lax.dot_general(rows_in, azim_table, contract_dims, preferred_element_typ...  6.11 us
    dot_general x1, matrix products, to_samples(): return jnp.dot(rows_in, azim_table, preferred_element_type=jnp.float32)  4.77 us
  transfers between devices with their start and end apart: 4, of which 0 were waited for; matrix products, arithmetic and copies ran while one was open for 9% of the time, Pallas kernels for 0%

commit v1 on v0

v1 whole, which is shorter than its diff:
```python
import math

import jax
import jax.numpy as jnp
import numpy as np
from jax import lax
from jax.experimental import pallas as pl
from jax.experimental.pallas import tpu as pltpu
from jax.sharding import PartitionSpec as P

NODES = 25
ROWS = 56
PITCH = 40
LANES = 128


def shifted(value, axis, steps):
    count = lax.axis_size(axis)
    initial, last = (max(0, -steps), min(count, count - steps))
    return lax.ppermute(value, axis, [(source, source + steps) for source in range(initial, last)])


def gll_tables():
    inner_root = math.sqrt(3.0 / 7.0)
    points = np.array([-1.0, -inner_root, 0.0, inner_root, 1.0])
    weights = np.array([0.1, 49.0 / 90.0, 32.0 / 45.0, 49.0 / 90.0, 0.1])
    legendre = (35.0 * points**4 - 30.0 * points**2 + 3.0) / 8.0
    derivative = np.zeros((5, 5))
    for target in range(5):
        for source in range(5):
            if target != source:
                derivative[target, source] = (
                    legendre[target] / legendre[source] / (points[target] - points[source])
                )
    derivative[0, 0] = -5.0
    derivative[4, 4] = 5.0
    return derivative, np.outer(weights, weights)


DERIV, QUAD = gll_tables()


def transform_tables():
    lane = np.arange(LANES)
    sample = 8 * (lane % 16) + lane // 16
    angle = 2.0 * np.pi * ((np.arange(LANES)[:, None] * sample[None, :]) % LANES) / LANES
    table = np.concatenate([np.cos(angle), -np.sin(angle)], axis=0) / 32.0
    turn = 2.0 * np.pi * np.arange(16)[:, None] * lane[None, :] / 2048.0
    twiddle = np.concatenate([np.cos(turn), np.sin(turn)], axis=0)
    return table, twiddle


def times_root(z, eighth, sign):
    re, im = z
    root = math.sqrt(0.5)
    if eighth == 0:
        return z
    if eighth == 1:
        return ((re - im) * root, (re + im) * root) if sign > 0 else ((re + im) * root, (im - re) * root)
    if eighth == 2:
        return (-im, re) if sign > 0 else (im, -re)
    return ((-re - im) * root, (re - im) * root) if sign > 0 else ((im - re) * root, (-re - im) * root)


def plus(x, y):
    return (x[0] + y[0], x[1] + y[1])


def minus(x, y):
    return (x[0] - y[0], x[1] - y[1])


def plus_turned(x, y, sign):
    return (x[0] - y[1], x[1] + y[0]) if sign > 0 else (x[0] + y[1], x[1] - y[0])


def dft4(a, b, c, d, sign):
    s, t, u, v = plus(a, c), minus(a, c), plus(b, d), minus(b, d)
    return [plus(s, u), plus_turned(t, v, sign), minus(s, u), plus_turned(t, v, -sign)]


def dft8(z, sign):
    even = dft4(z[0], z[2], z[4], z[6], sign)
    odd = dft4(z[1], z[3], z[5], z[7], sign)
    low, high = [], []
    for k in range(4):
        if k == 2:
            low.append(plus_turned(even[k], odd[k], sign))
            high.append(plus_turned(even[k], odd[k], -sign))
        else:
            turned = times_root(odd[k], k, sign)
            low.append(plus(even[k], turned))
            high.append(minus(even[k], turned))
    return low + high


def times_const(z, angle):
    c, s = math.cos(angle), math.sin(angle)
    return (z[0] * c - z[1] * s, z[0] * s + z[1] * c)


def spread(z):
    even = dft8(z, 1)
    odd = dft8([z[0]] + [times_const(z[m], math.pi * m / 8.0) for m in range(1, 8)], 1)
    return [(even, odd)[k % 2][k // 2] for k in range(16)]


def gathered(v):
    even = dft8(v[0::2], -1)
    odd = dft8(v[1::2], -1)
    return [plus(even[m], times_const(odd[m], -math.pi * m / 8.0) if m else odd[m]) for m in range(8)]


def centred(table, p):
    e0, o0, e1, o1, c = p[0] + p[4], p[0] - p[4], p[1] + p[3], p[1] - p[3], p[2]
    out = [None] * 5
    for i in range(2):
        t = table[i]
        odd = o0 * float(0.5 * (t[0] - t[4])) + o1 * float(0.5 * (t[1] - t[3]))
        even = e0 * float(0.5 * (t[0] + t[4])) + e1 * float(0.5 * (t[1] + t[3])) + c * float(t[2])
        out[i], out[4 - i] = odd + even, odd - even
    out[2] = o0 * float(table[2, 0]) + o1 * float(table[2, 1])
    return out


def swap_blocks(x):
    lane = lax.broadcasted_iota(jnp.int32, x[0].shape, 1)
    for bit in (8, 4, 2, 1):
        clear = (lane & bit) == 0
        for s in range(16):
            if s & bit:
                continue
            a, b = x[s], x[s | bit]
            x[s] = jnp.where(clear, a, pltpu.roll(b, bit, 1))
            x[s | bit] = jnp.where(clear, pltpu.roll(a, LANES - bit, 1), b)
    return x


def order_limit(bucket):
    return jnp.where(bucket == 0, 16, jnp.where(bucket == 1, 64, jnp.where(bucket == 2, 256, 1024)))


def stiffness_kernel(
    bucket_ref, blk_ref, band_ref, radius_ref, twiddle_ref, table_ref, back_ref, fwd_hbm, adj_hbm, mod_hbm,
    stiff_ref, waves_ref, blk_low_ref, blk_high_ref, band_low_ref, band_high_ref,
    field, mod, weight, stress, inv, sems,
):
    loads = [
        pltpu.make_async_copy(fwd_hbm, field.at[pl.ds(0, 400)], sems.at[0]),
        pltpu.make_async_copy(adj_hbm, field.at[pl.ds(400, 400)], sems.at[1]),
        pltpu.make_async_copy(mod_hbm, mod.at[pl.ds(0, 400)], sems.at[2]),
    ]
    for load in loads:
        load.start()
    limit = order_limit(bucket_ref[0, 0])
    lane8 = lax.broadcasted_iota(jnp.int32, (8, LANES), 1)
    orders = [(lane8 + 128 * a).astype(jnp.float32) for a in range(8)]

    row = lax.broadcasted_iota(jnp.int32, (ROWS, LANES), 0)
    node = jnp.where(row >= NODES, row - NODES, row)
    lane = lax.broadcasted_iota(jnp.int32, (ROWS, LANES), 1)
    radius = jnp.broadcast_to(radius_ref[0:1, :], (ROWS, LANES))
    radius = jnp.sum(jnp.where(lane == node, radius, 0.0), axis=1, keepdims=True)
    inv[...] = jnp.broadcast_to(1.0 / jnp.where(radius > 0.0, radius, 1.0), (ROWS, LANES))
    loads[0].wait()
    loads[1].wait()

    def forward(g, carry):
        inv_r = inv[pl.ds(pl.multiple_of(8 * g, 8), 8), :]
        base = 128 * g
        u, w = [], []
        for a in range(8):
            kept = (lane8 + 128 * a) < limit
            re = jnp.where(kept, field[pl.ds(base + a, 8, stride=16), :], 0.0)
            im = jnp.where(kept, field[pl.ds(base + 8 + a, 8, stride=16), :], 0.0)
            scale = orders[a]
            w.append((-(scale * im) * inv_r, (scale * re) * inv_r))
            u.append((re, im))
        res, ims = [], []
        for z in (u, w):
            z = [tuple(part.astype(jnp.bfloat16).astype(jnp.float32) for part in term) for term in z]
            for c, (re, im) in enumerate(spread(z)):
                if c:
                    cos, sin = twiddle_ref[c : c + 1, :], twiddle_ref[16 + c : 17 + c, :]
                    re, im = re * cos - im * sin, re * sin + im * cos
                res.append(re)
                ims.append(im)
        lhs = jnp.concatenate([jnp.concatenate(res, axis=0), jnp.concatenate(ims, axis=0)], axis=1)
        out = jnp.dot(lhs.astype(jnp.bfloat16), table_ref[...], preferred_element_type=jnp.float32)
        for t in range(2):
            for c in range(16):
                at = pl.multiple_of(ROWS * c + 8 * g, 8)
                waves_ref[t, pl.ds(at, 8), :] = out[128 * t + 8 * c : 128 * t + 8 * c + 8]
        return carry

    lax.fori_loop(0, ROWS // 8, forward, 0)
    loads[2].wait()

    def reorder(g, carry):
        x = swap_blocks([mod[pl.ds(128 * g + s, 8, stride=16), :] for s in range(16)])
        for c in range(16):
            weight[pl.ds(pl.multiple_of(PITCH * c + 8 * g, 8), 8), :] = x[c]
        return carry

    lax.fori_loop(0, 4, reorder, 0)

    def stencil(step, carry):
        half, f = step // 2, step % 2
        top = ROWS * 8 * half + NODES * f
        w = [
            [weight[pl.ds(PITCH * 8 * half + 5 * i + j, 8, stride=PITCH), :] * float(QUAD[i, j]) for j in range(5)]
            for i in range(5)
        ]
        p = [[waves_ref[0, pl.ds(top + 5 * i + j, 8, stride=ROWS), :] for j in range(5)] for i in range(5)]
        total = []
        for i in range(5):
            grad = centred(DERIV, p[i])
            total.append(centred(DERIV.T, [w[i][j] * grad[j] for j in range(5)]))
        for j in range(5):
            grad = centred(DERIV, [p[i][j] for i in range(5)])
            part = centred(DERIV.T, [w[i][j] * grad[i] for i in range(5)])
            for i in range(5):
                stress[0, pl.ds(top + 5 * i + j, 8, stride=ROWS), :] = total[i][j] + part[i]
        for i in range(5):
            for j in range(5):
                at = pl.ds(top + 5 * i + j, 8, stride=ROWS)
                stress[1, at, :] = w[i][j] * waves_ref[1, at, :]
        return carry

    lax.fori_loop(0, 4, stencil, 0)

    def backward(g, carry):
        inv_r = inv[pl.ds(pl.multiple_of(8 * g, 8), 8), :]
        rows = [
            stress[t, pl.ds(pl.multiple_of(ROWS * c + 8 * g, 8), 8), :] for t in range(2) for c in range(16)
        ]
        lhs = jnp.concatenate(rows, axis=0).astype(jnp.bfloat16)
        out = jnp.dot(lhs, back_ref[...], preferred_element_type=jnp.float32)
        terms = []
        for t in range(2):
            v = []
            for c in range(16):
                at = 128 * t + 8 * c
                re, im = out[at : at + 8, :LANES], out[at : at + 8, LANES:]
                if c:
                    cos, sin = twiddle_ref[c : c + 1, :], twiddle_ref[16 + c : 17 + c, :]
                    re, im = re * cos + im * sin, im * cos - re * sin
                v.append((re, im))
            terms.append(gathered(v))
        for a in range(8):
            kept = (lane8 + 128 * a) < limit
            scale = orders[a]
            re = terms[0][a][0] + (scale * terms[1][a][1]) * inv_r
            im = terms[0][a][1] - (scale * terms[1][a][0]) * inv_r
            stiff_ref[pl.ds(128 * g + a, 8, stride=16), :] = jnp.where(kept, re, 0.0)
            stiff_ref[pl.ds(128 * g + 8 + a, 8, stride=16), :] = jnp.where(kept, im, 0.0)
        return carry

    lax.fori_loop(0, ROWS // 8, backward, 0)

    for ids, side, slots, out_ref in (
        (blk_ref, 0, 8, blk_low_ref), (blk_ref, 1, 8, blk_high_ref),
        (band_ref, 0, 4, band_low_ref), (band_ref, 1, 4, band_high_ref),
    ):
        for k in range(slots):
            at = ids[side, k] * 16
            for f in range(2):
                out_ref[pl.ds((f * slots + k) * 16, 16), :] = stiff_ref[pl.ds(pl.multiple_of(at + 400 * f, 16), 16), :]


def local_kernel(
    bucket_ref, scale_ref, waves_ref, stiff_ref, fwd_ref, adj_ref, prev_fwd_ref, prev_adj_ref, kernel_ref,
    base_ref, out_ref, slab,
):
    limit = order_limit(bucket_ref[0, 0])
    slot = lax.broadcasted_iota(jnp.int32, (16, LANES), 0)
    order = lax.broadcasted_iota(jnp.int32, (16, LANES), 1) + 128 * (slot % 8)
    kept = order < limit

    def update(n, carry):
        growth = scale_ref[0, n]
        at = pl.multiple_of(16 * n, 16)
        for f, (disp, prev) in enumerate(((fwd_ref, prev_fwd_ref), (adj_ref, prev_adj_ref))):
            rows = pl.ds(at, 16)
            both = pl.ds(pl.multiple_of(at + 400 * f, 16), 16)
            value = 2.0 * disp[rows, :] - prev[rows, :] - growth * stiff_ref[both, :]
            base_ref[both, :] = jnp.where(kept, value, 0.0)
        return carry

    lax.fori_loop(0, NODES, update, 0, unroll=5)

    for half in range(2):
        top = ROWS * 8 * half
        p = [
            [[waves_ref[0, pl.ds(top + NODES * f + 5 * i + j, 8, stride=ROWS), :] for j in range(5)] for i in range(5)]
            for f in range(2)
        ]
        total = [
            [
                waves_ref[1, pl.ds(top + 5 * i + j, 8, stride=ROWS), :]
                * waves_ref[1, pl.ds(top + NODES + 5 * i + j, 8, stride=ROWS), :]
                for j in range(5)
            ]
            for i in range(5)
        ]
        for i in range(5):
            fwd, adj = centred(DERIV, p[0][i]), centred(DERIV, p[1][i])
            for j in range(5):
                total[i][j] = total[i][j] + fwd[j] * adj[j]
        for j in range(5):
            fwd, adj = (centred(DERIV, [p[f][i][j] for i in range(5)]) for f in range(2))
            for i in range(5):
                slab[pl.ds(PITCH * 8 * half + 5 * i + j, 8, stride=PITCH), :] = (
                    total[i][j] + fwd[i] * adj[i]
                ) * float(QUAD[i, j])

    def finish(g, carry):
        x = swap_blocks([slab[pl.ds(pl.multiple_of(PITCH * c + 8 * g, 8), 8), :] for c in range(16)])
        for s in range(16):
            at = pl.ds(128 * g + s, 8, stride=16)
            out_ref[at, :] = kernel_ref[at, :] - x[s]
        return carry

    lax.fori_loop(0, 3, finish, 0)
    x = swap_blocks([slab[pl.ds(PITCH * c + 24, 1), :] for c in range(16)])
    for s in range(16):
        out_ref[pl.ds(384 + s, 1), :] = kernel_ref[pl.ds(384 + s, 1), :] - x[s]


def join_kernel(
    bucket_ref, count_ref, blk_ref, band_ref, scale_ref, base_ref, below_ref, above_ref, band_below_ref, band_above_ref,
    fwd_ref, adj_ref,
):
    limit = order_limit(bucket_ref[0, 0])
    slot = lax.broadcasted_iota(jnp.int32, (16, LANES), 0)
    order = lax.broadcasted_iota(jnp.int32, (16, LANES), 1) + 128 * (slot % 8)
    kept = order < limit
    outs = (fwd_ref, adj_ref)
    for f in range(2):
        outs[f][...] = base_ref[pl.ds(400 * f, 400), :]
    for side, ids, lane_side, slots, got in (
        (0, blk_ref, 0, 8, below_ref), (1, blk_ref, 1, 8, above_ref),
        (2, band_ref, 0, 4, band_below_ref), (3, band_ref, 1, 4, band_above_ref),
    ):
        for k in range(slots):
            node = ids[lane_side, k]
            take = jnp.logical_and(kept, k < count_ref[0, side])
            growth = scale_ref[0, node]
            at = pl.ds(pl.multiple_of(16 * node, 16), 16)
            for f in range(2):
                step = growth * got[pl.ds((f * slots + k) * 16, 16), :]
                outs[f][at, :] = outs[f][at, :] - jnp.where(take, step, 0.0)


def smem():
    return pl.BlockSpec(memory_space=pltpu.SMEM)


def vmem():
    return pl.BlockSpec(memory_space=pltpu.VMEM)


def anywhere():
    return pl.BlockSpec(memory_space=pl.ANY)


def shape(*dims):
    return jax.ShapeDtypeStruct(dims, jnp.float32)


def per_device(
    disp_fwd, prev_fwd, disp_adj, prev_adj, modulus, radius, step_scale, kernel_in, buckets, halo_count,
    blk_nodes, band_nodes,
):
    flat = lambda value: value.reshape(16 * NODES, LANES)
    table, twiddle = transform_tables()
    fwd, adj = flat(disp_fwd), flat(disp_adj)
    bucket, blk, band = buckets.reshape(1, 1), blk_nodes.reshape(2, 8), band_nodes.reshape(2, 4)
    scale = step_scale.reshape(1, NODES)
    line = jnp.pad(radius.reshape(1, NODES), ((0, 0), (0, LANES - NODES)))
    stiff, waves, blk_low, blk_high, band_low, band_high = pl.pallas_call(
        stiffness_kernel,
        out_shape=(
            shape(16 * ROWS, LANES), shape(2, 16 * ROWS, LANES), shape(256, LANES), shape(256, LANES),
            shape(128, LANES), shape(128, LANES),
        ),
        in_specs=[smem(), smem(), smem(), vmem(), vmem(), vmem(), vmem(), anywhere(), anywhere(), anywhere()],
        out_specs=(vmem(),) * 6,
        scratch_shapes=[
            pltpu.VMEM((16 * ROWS, LANES), jnp.float32),
            pltpu.VMEM((512, LANES), jnp.float32),
            pltpu.VMEM((16 * PITCH, LANES), jnp.float32),
            pltpu.VMEM((2, 16 * ROWS, LANES), jnp.float32),
            pltpu.VMEM((ROWS, LANES), jnp.float32),
            pltpu.SemaphoreType.DMA((3,)),
        ],
        cost_estimate=pl.CostEstimate(flops=500_000_000, bytes_accessed=3_000_000, transcendentals=0),
        name="stiffness",
    )(
        bucket, blk, band, line, jnp.asarray(twiddle, jnp.float32), jnp.asarray(table, jnp.bfloat16),
        jnp.asarray(table.T, jnp.bfloat16), fwd, adj, flat(modulus),
    )
    from_below = shifted(blk_high, "blk", 1)
    from_above = shifted(blk_low, "blk", -1)
    band_below = shifted(band_high, "band", 1)
    band_above = shifted(band_low, "band", -1)
    base, kernel_out = pl.pallas_call(
        local_kernel,
        out_shape=(shape(800, LANES), shape(400, LANES)),
        in_specs=[smem(), smem()] + [vmem()] * 7,
        out_specs=(vmem(), vmem()),
        scratch_shapes=[pltpu.VMEM((16 * PITCH, LANES), jnp.float32)],
        cost_estimate=pl.CostEstimate(flops=100_000_000, bytes_accessed=3_000_000, transcendentals=0),
        name="local",
    )(bucket, scale, waves, stiff, fwd, adj, flat(prev_fwd), flat(prev_adj), flat(kernel_in))
    next_fwd, next_adj = pl.pallas_call(
        join_kernel,
        out_shape=(shape(400, LANES), shape(400, LANES)),
        in_specs=[smem()] * 5 + [vmem()] * 5,
        out_specs=(vmem(), vmem()),
        cost_estimate=pl.CostEstimate(flops=1_000_000, bytes_accessed=1_500_000, transcendentals=0),
        name="join",
    )(
        bucket, halo_count.reshape(1, 4), blk, band, scale, base, from_below, from_above, band_below, band_above
    )
    return tuple(value.reshape(disp_fwd.shape) for value in (next_fwd, next_adj, kernel_out))


def solution(mesh):
    wide = P("blk", "band", None, None)
    line = P("blk", "band", None)
    in_specs = (wide,) * 5 + (line, line, wide, P("blk", "band"), line, wide, wide)
    return jax.shard_map(
        per_device, mesh=mesh, in_specs=in_specs, out_specs=(wide, wide, wide), check_vma=False
    )
```

time: 137 us -> 48.6 us (0.35)
  the two profiles are of different devices: /device:TPU:58 before, /device:TPU:7 now
where the time goes in v1:
time: 48.6 us; the launch traced here: 48.3 us
  starting transfers between devices  27.1 us (56%)
  Pallas kernels  14.2 us (29%)
  waiting for transfers between devices  3.84 us (8%)
  local copies, waits for them, and re-layouts  1.88 us (4%)
  between operations  1.35 us (3%)
    ppermute x4, starting transfers between devices, shifted(): lax.ppermute(value, axis, [(source, source + steps) for source in range(i...  27.1 us
    pallas_call x1, Pallas kernels, per_device(): pl.pallas_call(stiffness_kernel, out_shape=(shape(16 * ROWS, LANES), shap...  8.22 us
    pallas_call x1, Pallas kernels, per_device(): pl.pallas_call(local_kernel, out_shape=(shape(800, LANES), shape(400, LAN...  3.93 us
    ppermute x4, waiting for transfers between devices, shifted(): lax.ppermute(value, axis, [(source, source + steps) for source in range(i...  3.84 us
    pallas_call x1, Pallas kernels, per_device(): pl.pallas_call(join_kernel, out_shape=(shape(400, LANES), shape(400, LANE...  2.03 us
    unnamed x10, local copies, waits for them, and re-layouts  1.37 us
  transfers between devices with their start and end apart: 4, of which 1 were waited for; matrix products, arithmetic and copies ran while one was open for 0% of the time, Pallas kernels for 8%

profile of v1, /device:TPU:7, one launch (start us, length us, event | category | flops | bytes accessed | tf_op | source)
XLA Modules:
  0.0 48.3 jit_solution(16792804265329471852)
XLA Ops:
  1.3 0.0 copy-start.4
  1.3 0.6 %copy-done.4 = f32[1,1,25]{2,1,0:T(1,128)S(1)} copy-done((f32[1,1,25]{2,1,0:T(1,128)S(1)}, f32[1,1,25]{2,1,0:T(1,128)}, u32[]{:S(2)}) %copy-start.4) | copy-done | bytes 124
  1.9 0.5 %pad.4.radius_ref = f32[1,128]{1,0:T(1,128)} pad(f32[1,25]{1,0:T(1,128)S(1)} %bitcast.32, f32[]{:T(128)} %constant.8.clone.1), padding=0_0x0_103 | pad | bytes 616 | tf_op jit(solution)/shard_map/jit(_pad)/pad | solution.py:380
  2.4 8.2 %stiffness.1 = (f32[896,128]{1,0:T(8,128)}, f32[2,896,128]{2,1,0:T(8,128)}, f32[256,128]{1,0:T(8,128)}, f32[256,128]{1,0:T(8,128)}, f32[128,128]{1,0:T(8,128)}, /*index=5*/f32[128,128]{1,0:T(8,128)}) custom-call(s32[1,1]{1,0:T(1,128)S(6)} %copy.24.bucket_ref, s32[2,8]{1,0:T(2,128)} %bitcast.23, s32[2,4]{1,0:T(2,128)} %bitcast.25, f32[1,128]{1,0:T(1,128)} %pad.4.radius_ref, ...), custom_call_target="tpu_custom_call" | custom-call | flops 500000000 | bytes 3000000 | tf_op jit(solution)/shard_map/stiffness/pallas_call | solution.py:381
  10.7 4.0 %collective-permute-start = (f32[256,128]{1,0:T(8,128)}, f32[256,128]{1,0:T(8,128)S(1)}, u32[]{:S(2)}, u32[]{:S(2)}) collective-permute-start(f32[256,128]{1,0:T(8,128)} %get-tuple-element.16), channel_id=1, source_target_pairs={{0,4},{4,8},{8,12},{12,16},{16,20},{20,24},{24,28},{28,32},{32,36}... | collective-permute-start | bytes 393224 | tf_op jit(solution)/shard_map/ppermute | solution.py:20
  14.7 15.5 %collective-permute-start.1 = (f32[256,128]{1,0:T(8,128)}, f32[256,128]{1,0:T(8,128)S(1)}, u32[]{:S(2)}, u32[]{:S(2)}) collective-permute-start(f32[256,128]{1,0:T(8,128)} %get-tuple-element.17), channel_id=1, source_target_pairs={{4,0},{8,4},{12,8},{16,12},{20,16},{24,20},{28,24},{32,28},{36,32}... | collective-permute-start | bytes 393224 | tf_op jit(solution)/shard_map/ppermute | solution.py:20
  30.2 5.6 %collective-permute-start.2 = (f32[128,128]{1,0:T(8,128)}, f32[128,128]{1,0:T(8,128)S(1)}, u32[]{:S(2)}, u32[]{:S(2)}) collective-permute-start(f32[128,128]{1,0:T(8,128)} %get-tuple-element.18), channel_id=1, source_target_pairs={{0,1},{1,2},{2,3},{4,5},{5,6},{6,7},{8,9},{9,10},{10,11},{12,13},{... | collective-permute-start | bytes 196616 | tf_op jit(solution)/shard_map/ppermute | solution.py:20
  35.8 1.9 %collective-permute-start.3 = (f32[128,128]{1,0:T(8,128)}, f32[128,128]{1,0:T(8,128)S(1)}, u32[]{:S(2)}, u32[]{:S(2)}) collective-permute-start(f32[128,128]{1,0:T(8,128)} %get-tuple-element.19), channel_id=1, source_target_pairs={{1,0},{2,1},{3,2},{5,4},{6,5},{7,6},{9,8},{10,9},{11,10},{13,12},{... | collective-permute-start | bytes 196616 | tf_op jit(solution)/shard_map/ppermute | solution.py:20
  37.8 3.9 %local.1 = (f32[800,128]{1,0:T(8,128)}, f32[400,128]{1,0:T(8,128)}) custom-call(s32[1,1]{1,0:T(1,128)S(6)} %copy.24.bucket_ref, f32[1,25]{1,0:T(1,128)} %bitcast.21, f32[2,896,128]{2,1,0:T(8,128)} %get-tuple-element.13.waves_ref, f32[896,128]{1,0:T(8,128)} %get-tuple-element.14.stiff_ref, f32[400,128]{1,0:T(8,128)} %bitcast.15, f32[400,128]{1,0:T(8,128)} %bitcast.17, ...), custom_call_target="tpu_custom_call" | custom-call | flops 100000000 | bytes 3000000 | tf_op jit(solution)/shard_map/local/pallas_call | solution.py:407
  41.7 0.0 collective-permute-done.2.band_below_ref
  41.7 0.0 copy-start.2
  41.7 3.8 %collective-permute-done.3.band_above_ref = f32[128,128]{1,0:T(8,128)S(1)} collective-permute-done((f32[128,128]{1,0:T(8,128)}, f32[128,128]{1,0:T(8,128)S(1)}, u32[]{:S(2)}, u32[]{:S(2)}) %collective-permute-start.3) | collective-permute-done | bytes 65568 | tf_op jit(solution)/shard_map/ppermute | solution.py:20
  45.5 0.0 copy-start.3
  45.5 0.0 collective-permute-done.below_ref
  45.5 0.0 copy-start
  45.5 0.0 collective-permute-done.1.above_ref
  45.6 0.0 copy-start.1
  45.6 0.0 copy-done.2
  45.6 0.6 %copy-done.3 = f32[128,128]{1,0:T(8,128)} copy-done((f32[128,128]{1,0:T(8,128)}, f32[128,128]{1,0:T(8,128)S(1)}, u32[]{:S(2)}) %copy-start.3) | copy-done | bytes 65560
  46.2 0.1 copy-done
  46.2 0.1 copy-done.1
  46.3 2.0 %join.1 = (f32[400,128]{1,0:T(8,128)}, f32[400,128]{1,0:T(8,128)}) custom-call(s32[1,1]{1,0:T(1,128)S(6)} %copy.24.bucket_ref, s32[1,4]{1,0:T(1,128)} %bitcast.27, s32[2,8]{1,0:T(2,128)} %bitcast.24, s32[2,4]{1,0:T(2,128)} %bitcast.26, f32[1,25]{1,0:T(1,128)} %bitcast.22, f32[800,128]{1,0:T(8,128)} %get-tuple-element.15.base_ref, f32[256,128]{1,0:T(8,128)} %copy-done, ...), custom_call_target="tpu_custom_call" | custom-call | flops 1000000 | bytes 1500000 | tf_op jit(solution)/shard_map/join/pallas_call | solution.py:416
Async XLA Ops:
  1.3 0.7 %copy-start.4 = (f32[1,1,25]{2,1,0:T(1,128)S(1)}, f32[1,1,25]{2,1,0:T(1,128)}, u32[]{:S(2)}) copy-start(f32[1,1,25]{2,1,0:T(1,128)} %param.20) | copy-start | bytes 304
  10.7 34.9 %collective-permute-start = (f32[256,128]{1,0:T(8,128)}, f32[256,128]{1,0:T(8,128)S(1)}, u32[]{:S(2)}, u32[]{:S(2)}) collective-permute-start(f32[256,128]{1,0:T(8,128)} %get-tuple-element.16), channel_id=1, source_target_pairs={{0,4},{4,8},{8,12},{12,16},{16,20},{20,24},{24,28},{28,32},{32,36}... | collective-permute-start | bytes 393224 | tf_op jit(solution)/shard_map/ppermute | solution.py:20
  14.7 30.8 %collective-permute-start.1 = (f32[256,128]{1,0:T(8,128)}, f32[256,128]{1,0:T(8,128)S(1)}, u32[]{:S(2)}, u32[]{:S(2)}) collective-permute-start(f32[256,128]{1,0:T(8,128)} %get-tuple-element.17), channel_id=1, source_target_pairs={{4,0},{8,4},{12,8},{16,12},{20,16},{24,20},{28,24},{32,28},{36,32}... | collective-permute-start | bytes 393224 | tf_op jit(solution)/shard_map/ppermute | solution.py:20
  30.2 11.5 %collective-permute-start.2 = (f32[128,128]{1,0:T(8,128)}, f32[128,128]{1,0:T(8,128)S(1)}, u32[]{:S(2)}, u32[]{:S(2)}) collective-permute-start(f32[128,128]{1,0:T(8,128)} %get-tuple-element.18), channel_id=1, source_target_pairs={{0,1},{1,2},{2,3},{4,5},{5,6},{6,7},{8,9},{9,10},{10,11},{12,13},{... | collective-permute-start | bytes 196616 | tf_op jit(solution)/shard_map/ppermute | solution.py:20
  35.8 9.7 %collective-permute-start.3 = (f32[128,128]{1,0:T(8,128)}, f32[128,128]{1,0:T(8,128)S(1)}, u32[]{:S(2)}, u32[]{:S(2)}) collective-permute-start(f32[128,128]{1,0:T(8,128)} %get-tuple-element.19), channel_id=1, source_target_pairs={{1,0},{2,1},{3,2},{5,4},{6,5},{7,6},{9,8},{10,9},{11,10},{13,12},{... | collective-permute-start | bytes 196616 | tf_op jit(solution)/shard_map/ppermute | solution.py:20
  41.7 3.9 %copy-start.2 = (f32[128,128]{1,0:T(8,128)}, f32[128,128]{1,0:T(8,128)S(1)}, u32[]{:S(2)}) copy-start(f32[128,128]{1,0:T(8,128)S(1)} %collective-permute-done.2.band_below_ref) | copy-start | bytes 196612
  45.5 0.6 %copy-start.3 = (f32[128,128]{1,0:T(8,128)}, f32[128,128]{1,0:T(8,128)S(1)}, u32[]{:S(2)}) copy-start(f32[128,128]{1,0:T(8,128)S(1)} %collective-permute-done.3.band_above_ref) | copy-start | bytes 196612
  45.5 0.7 %copy-start = (f32[256,128]{1,0:T(8,128)}, f32[256,128]{1,0:T(8,128)S(1)}, u32[]{:S(2)}) copy-start(f32[256,128]{1,0:T(8,128)S(1)} %collective-permute-done.below_ref) | copy-start | bytes 393220
  45.6 0.7 %copy-start.1 = (f32[256,128]{1,0:T(8,128)}, f32[256,128]{1,0:T(8,128)S(1)}, u32[]{:S(2)}) copy-start(f32[256,128]{1,0:T(8,128)S(1)} %collective-permute-done.1.above_ref) | copy-start | bytes 393220

commit v2 on v1

--- a/solution.py
+++ b/solution.py
@@ -8,16 +8,12 @@
 from jax.experimental.pallas import tpu as pltpu
 from jax.sharding import PartitionSpec as P
 
+
 NODES = 25
 ROWS = 56
 PITCH = 40
+RUN = 12
 LANES = 128
-
-
-def shifted(value, axis, steps):
-    count = lax.axis_size(axis)
-    initial, last = (max(0, -steps), min(count, count - steps))
-    return lax.ppermute(value, axis, [(source, source + steps) for source in range(initial, last)])
 
 
 def gll_tables():
@@ -140,30 +136,96 @@
     return jnp.where(bucket == 0, 16, jnp.where(bucket == 1, 64, jnp.where(bucket == 2, 256, 1024)))
 
 
+def device_role():
+    blk, band = lax.axis_index("blk"), lax.axis_index("band")
+    return lax.rem(blk, RUN) == 0, lax.rem(blk, 2), lax.rem(band, 2)
+
+
+def finish_locally(limit, scale_ref, waves_ref, stiff_ref, field_ref, late_ref, base_ref, slab, kout):
+    slot = lax.broadcasted_iota(jnp.int32, (16, LANES), 0)
+    order = lax.broadcasted_iota(jnp.int32, (16, LANES), 1) + 128 * (slot % 8)
+    kept = order < limit
+
+    def update(n, carry):
+        growth = scale_ref[0, n]
+        for f in range(2):
+            rows = pl.ds(pl.multiple_of(16 * n + 400 * f, 16), 16)
+            value = 2.0 * field_ref[rows, :] - late_ref[rows, :] - growth * stiff_ref[rows, :]
+            base_ref[rows, :] = jnp.where(kept, value, 0.0)
+        return carry
+
+    lax.fori_loop(0, NODES, update, 0, unroll=5)
+
+    def products(half, carry):
+        top = ROWS * 8 * half
+        p = [
+            [[waves_ref[0, pl.ds(top + NODES * f + 5 * i + j, 8, stride=ROWS), :] for j in range(5)] for i in range(5)]
+            for f in range(2)
+        ]
+        total = [
+            [
+                waves_ref[1, pl.ds(top + 5 * i + j, 8, stride=ROWS), :]
+                * waves_ref[1, pl.ds(top + NODES + 5 * i + j, 8, stride=ROWS), :]
+                for j in range(5)
+            ]
+            for i in range(5)
+        ]
+        for i in range(5):
+            fwd, adj = centred(DERIV, p[0][i]), centred(DERIV, p[1][i])
+            for j in range(5):
+                total[i][j] = total[i][j] + fwd[j] * adj[j]
+        for j in range(5):
+            fwd, adj = (centred(DERIV, [p[f][i][j] for i in range(5)]) for f in range(2))
+            for i in range(5):
+                slab[pl.ds(PITCH * 8 * half + 5 * i + j, 8, stride=PITCH), :] = (
+                    total[i][j] + fwd[i] * adj[i]
+                ) * float(QUAD[i, j])
+        return carry
+
+    lax.fori_loop(0, 2, products, 0, unroll=True)
+
+    def finish(g, carry):
+        x = swap_blocks([slab[pl.ds(pl.multiple_of(PITCH * c + 8 * g, 8), 8), :] for c in range(16)])
+        for s in range(16):
+            at = 128 * g + s
+            kout[pl.ds(at, 8, stride=16), :] = late_ref[pl.ds(800 + at, 8, stride=16), :] - x[s]
+        return carry
+
+    lax.fori_loop(0, 4, finish, 0, unroll=True)
+
+
 def stiffness_kernel(
-    bucket_ref, blk_ref, band_ref, radius_ref, twiddle_ref, table_ref, back_ref, fwd_hbm, adj_hbm, mod_hbm,
-    stiff_ref, waves_ref, blk_low_ref, blk_high_ref, band_low_ref, band_high_ref,
-    field, mod, weight, stress, inv, sems,
+    bucket_ref, radius_ref, scale_ref, blk_ref, band_ref, twiddle_hbm, table_hbm, back_hbm, fwd_hbm, adj_hbm, mod_hbm,
+    prev_fwd_hbm, prev_adj_hbm, kernel_hbm,
+    stiff_ref, waves_ref, field, late, base_ref, odd_hbm, even_hbm, chip_hbm, far_hbm, out_hbm,
+    mod, weight, stress, inv, twiddle_ref, table_ref, back_ref, slab, kout, odd_ref, even_ref, chip_ref, far_ref, sems,
 ):
     loads = [
-        pltpu.make_async_copy(fwd_hbm, field.at[pl.ds(0, 400)], sems.at[0]),
-        pltpu.make_async_copy(adj_hbm, field.at[pl.ds(400, 400)], sems.at[1]),
-        pltpu.make_async_copy(mod_hbm, mod.at[pl.ds(0, 400)], sems.at[2]),
+        pltpu.make_async_copy(source, target, sems.at[i])
+        for i, (source, target) in enumerate((
+            (fwd_hbm, field.at[pl.ds(0, 400)]), (adj_hbm, field.at[pl.ds(400, 400)]), (twiddle_hbm, twiddle_ref),
+            (table_hbm, table_ref), (mod_hbm, mod.at[pl.ds(0, 400)]), (back_hbm, back_ref),
+            (prev_fwd_hbm, late.at[pl.ds(0, 400)]), (prev_adj_hbm, late.at[pl.ds(400, 400)]),
+            (kernel_hbm, late.at[pl.ds(800, 400)]),
+        ))
     ]
-    for load in loads:
+    for load in loads[:6]:
         load.start()
     limit = order_limit(bucket_ref[0, 0])
+    first, odd, upper = device_role()
     lane8 = lax.broadcasted_iota(jnp.int32, (8, LANES), 1)
     orders = [(lane8 + 128 * a).astype(jnp.float32) for a in range(8)]
 
-    row = lax.broadcasted_iota(jnp.int32, (ROWS, LANES), 0)
-    node = jnp.where(row >= NODES, row - NODES, row)
-    lane = lax.broadcasted_iota(jnp.int32, (ROWS, LANES), 1)
-    radius = jnp.broadcast_to(radius_ref[0:1, :], (ROWS, LANES))
-    radius = jnp.sum(jnp.where(lane == node, radius, 0.0), axis=1, keepdims=True)
-    inv[...] = jnp.broadcast_to(1.0 / jnp.where(radius > 0.0, radius, 1.0), (ROWS, LANES))
-    loads[0].wait()
-    loads[1].wait()
+    inv[pl.ds(ROWS - 8, 8), :] = jnp.ones((8, LANES), jnp.float32)
+    for n in range(NODES):
+        line = jnp.full((1, LANES), radius_ref[0, n], jnp.float32)
+        inv[pl.ds(n, 1), :] = line
+        inv[pl.ds(NODES + n, 1), :] = line
+    inv[...] = 1.0 / inv[...]
+    for load in loads[:4]:
+        load.wait()
+    for load in loads[6:]:
+        load.start()
 
     def forward(g, carry):
         inv_r = inv[pl.ds(pl.multiple_of(8 * g, 8), 8), :]
@@ -193,8 +255,7 @@
                 waves_ref[t, pl.ds(at, 8), :] = out[128 * t + 8 * c : 128 * t + 8 * c + 8]
         return carry
 
-    lax.fori_loop(0, ROWS // 8, forward, 0)
-    loads[2].wait()
+    loads[4].wait()
 
     def reorder(g, carry):
         x = swap_blocks([mod[pl.ds(128 * g + s, 8, stride=16), :] for s in range(16)])
@@ -202,7 +263,8 @@
             weight[pl.ds(pl.multiple_of(PITCH * c + 8 * g, 8), 8), :] = x[c]
         return carry
 
-    lax.fori_loop(0, 4, reorder, 0)
+    lax.fori_loop(0, 4, lambda g, carry: reorder(g, forward(g, carry)), 0, unroll=True)
+    lax.fori_loop(4, ROWS // 8, forward, 0, unroll=True)
 
     def stencil(step, carry):
         half, f = step // 2, step % 2
@@ -227,7 +289,8 @@
                 stress[1, at, :] = w[i][j] * waves_ref[1, at, :]
         return carry
 
-    lax.fori_loop(0, 4, stencil, 0)
+    lax.fori_loop(0, 4, stencil, 0, unroll=True)
+    loads[5].wait()
 
     def backward(g, carry):
         inv_r = inv[pl.ds(pl.multiple_of(8 * g, 8), 8), :]
@@ -256,99 +319,77 @@
             stiff_ref[pl.ds(128 * g + 8 + a, 8, stride=16), :] = jnp.where(kept, im, 0.0)
         return carry
 
-    lax.fori_loop(0, ROWS // 8, backward, 0)
-
-    for ids, side, slots, out_ref in (
-        (blk_ref, 0, 8, blk_low_ref), (blk_ref, 1, 8, blk_high_ref),
-        (band_ref, 0, 4, band_low_ref), (band_ref, 1, 4, band_high_ref),
+    lax.fori_loop(0, ROWS // 8, backward, 0, unroll=True)
+
+    sends = []
+    for ids, side, slots, ref, hbm in (
+        (blk_ref, 1 - odd, 8, even_ref, even_hbm), (blk_ref, odd, 8, odd_ref, odd_hbm),
+        (band_ref, upper, 4, far_ref, far_hbm), (band_ref, 1 - upper, 4, chip_ref, chip_hbm),
     ):
         for k in range(slots):
             at = ids[side, k] * 16
             for f in range(2):
-                out_ref[pl.ds((f * slots + k) * 16, 16), :] = stiff_ref[pl.ds(pl.multiple_of(at + 400 * f, 16), 16), :]
+                ref[pl.ds((f * slots + k) * 16, 16), :] = stiff_ref[pl.ds(pl.multiple_of(at + 400 * f, 16), 16), :]
+        sends.append(pltpu.make_async_copy(ref, hbm, sems.at[10 + len(sends)]))
+        sends[-1].start()
+    for load in loads[6:]:
+        load.wait()
+
+    @pl.when(first)
+    def _():
+        finish_locally(limit, scale_ref, waves_ref, stiff_ref, field, late, base_ref, slab, kout)
+        store = pltpu.make_async_copy(kout.at[pl.ds(0, 400)], out_hbm, sems.at[9])
+        store.start()
+        store.wait()
+
+    for send in sends:
+        send.wait()
 
 
 def local_kernel(
-    bucket_ref, scale_ref, waves_ref, stiff_ref, fwd_ref, adj_ref, prev_fwd_ref, prev_adj_ref, kernel_ref,
-    base_ref, out_ref, slab,
+    bucket_ref, scale_ref, waves_ref, stiff_ref, field_ref, late_ref, base_in, out_in,
+    base_ref, out_hbm, slab, kout, sem,
 ):
-    limit = order_limit(bucket_ref[0, 0])
-    slot = lax.broadcasted_iota(jnp.int32, (16, LANES), 0)
-    order = lax.broadcasted_iota(jnp.int32, (16, LANES), 1) + 128 * (slot % 8)
-    kept = order < limit
-
-    def update(n, carry):
-        growth = scale_ref[0, n]
-        at = pl.multiple_of(16 * n, 16)
-        for f, (disp, prev) in enumerate(((fwd_ref, prev_fwd_ref), (adj_ref, prev_adj_ref))):
-            rows = pl.ds(at, 16)
-            both = pl.ds(pl.multiple_of(at + 400 * f, 16), 16)
-            value = 2.0 * disp[rows, :] - prev[rows, :] - growth * stiff_ref[both, :]
-            base_ref[both, :] = jnp.where(kept, value, 0.0)
-        return carry
-
-    lax.fori_loop(0, NODES, update, 0, unroll=5)
-
-    for half in range(2):
-        top = ROWS * 8 * half
-        p = [
-            [[waves_ref[0, pl.ds(top + NODES * f + 5 * i + j, 8, stride=ROWS), :] for j in range(5)] for i in range(5)]
-            for f in range(2)
-        ]
-        total = [
-            [
-                waves_ref[1, pl.ds(top + 5 * i + j, 8, stride=ROWS), :]
-                * waves_ref[1, pl.ds(top + NODES + 5 * i + j, 8, stride=ROWS), :]
-                for j in range(5)
-            ]
-            for i in range(5)
-        ]
-        for i in range(5):
-            fwd, adj = centred(DERIV, p[0][i]), centred(DERIV, p[1][i])
-            for j in range(5):
-                total[i][j] = total[i][j] + fwd[j] * adj[j]
-        for j in range(5):
-            fwd, adj = (centred(DERIV, [p[f][i][j] for i in range(5)]) for f in range(2))
-            for i in range(5):
-                slab[pl.ds(PITCH * 8 * half + 5 * i + j, 8, stride=PITCH), :] = (
-                    total[i][j] + fwd[i] * adj[i]
-                ) * float(QUAD[i, j])
-
-    def finish(g, carry):
-        x = swap_blocks([slab[pl.ds(pl.multiple_of(PITCH * c + 8 * g, 8), 8), :] for c in range(16)])
-        for s in range(16):
-            at = pl.ds(128 * g + s, 8, stride=16)
-            out_ref[at, :] = kernel_ref[at, :] - x[s]
-        return carry
-
-    lax.fori_loop(0, 3, finish, 0)
-    x = swap_blocks([slab[pl.ds(PITCH * c + 24, 1), :] for c in range(16)])
-    for s in range(16):
-        out_ref[pl.ds(384 + s, 1), :] = kernel_ref[pl.ds(384 + s, 1), :] - x[s]
+    first, _, _ = device_role()
+
+    @pl.when(first)
+    def _():
+        base_ref[...] = base_in[...]
+
+    @pl.when(jnp.logical_not(first))
+    def _():
+        limit = order_limit(bucket_ref[0, 0])
+        finish_locally(limit, scale_ref, waves_ref, stiff_ref, field_ref, late_ref, base_ref, slab, kout)
+        store = pltpu.make_async_copy(kout.at[pl.ds(0, 400)], out_hbm, sem)
+        store.start()
+        store.wait()
 
 
 def join_kernel(
-    bucket_ref, count_ref, blk_ref, band_ref, scale_ref, base_ref, below_ref, above_ref, band_below_ref, band_above_ref,
+    bucket_ref, count_ref, blk_ref, band_ref, scale_ref, base_ref, odd_ref, even_ref, chip_ref, far_ref, next_ref, last_ref,
     fwd_ref, adj_ref,
 ):
     limit = order_limit(bucket_ref[0, 0])
+    _, odd, upper = device_role()
     slot = lax.broadcasted_iota(jnp.int32, (16, LANES), 0)
     order = lax.broadcasted_iota(jnp.int32, (16, LANES), 1) + 128 * (slot % 8)
     kept = order < limit
     outs = (fwd_ref, adj_ref)
     for f in range(2):
         outs[f][...] = base_ref[pl.ds(400 * f, 400), :]
-    for side, ids, lane_side, slots, got in (
-        (0, blk_ref, 0, 8, below_ref), (1, blk_ref, 1, 8, above_ref),
-        (2, band_ref, 0, 4, band_below_ref), (3, band_ref, 1, 4, band_above_ref),
+    for start, ids, side, slots, got in (
+        (0, blk_ref, odd, 8, (odd_ref,)), (0, blk_ref, 1 - odd, 8, (even_ref, next_ref)),
+        (2, band_ref, 1 - upper, 4, (chip_ref,)), (2, band_ref, upper, 4, (far_ref, last_ref)),
     ):
+        count = count_ref[0, start + side]
         for k in range(slots):
-            node = ids[lane_side, k]
-            take = jnp.logical_and(kept, k < count_ref[0, side])
+            node = ids[side, k]
+            take = jnp.logical_and(kept, k < count)
             growth = scale_ref[0, node]
             at = pl.ds(pl.multiple_of(16 * node, 16), 16)
             for f in range(2):
-                step = growth * got[pl.ds((f * slots + k) * 16, 16), :]
+                rows = pl.ds((f * slots + k) * 16, 16)
+                step = growth * sum(ref[rows, :] for ref in got)
                 outs[f][at, :] = outs[f][at, :] - jnp.where(take, step, 0.0)
 
 
@@ -364,8 +405,19 @@
     return pl.BlockSpec(memory_space=pl.ANY)
 
 
+def near(*dims):
+    return pltpu.VMEM(dims, jnp.float32)
+
+
 def shape(*dims):
     return jax.ShapeDtypeStruct(dims, jnp.float32)
+
+
+def swap(value, chosen):
+    bands = lax.axis_size("band")
+    pairs = [(b * bands + z, c * bands + y) for (b, z), (c, y) in chosen]
+    pairs = sorted(pairs + [(target, source) for source, target in pairs])
+    return lax.ppermute(value, ("blk", "band"), pairs)
 
 
 def per_device(
@@ -373,55 +425,63 @@
     blk_nodes, band_nodes,
 ):
     flat = lambda value: value.reshape(16 * NODES, LANES)
+    close = lambda value: pltpu.with_memory_space_constraint(value, pltpu.VMEM)
     table, twiddle = transform_tables()
-    fwd, adj = flat(disp_fwd), flat(disp_adj)
     bucket, blk, band = buckets.reshape(1, 1), blk_nodes.reshape(2, 8), band_nodes.reshape(2, 4)
     scale = step_scale.reshape(1, NODES)
-    line = jnp.pad(radius.reshape(1, NODES), ((0, 0), (0, LANES - NODES)))
-    stiff, waves, blk_low, blk_high, band_low, band_high = pl.pallas_call(
+    blks, bands = lax.axis_size("blk"), lax.axis_size("band")
+    f32 = lambda *dims: pltpu.VMEM(dims, jnp.float32)
+    stiff, waves, field, late, base, odd, even, chip, far, kernel_out = pl.pallas_call(
         stiffness_kernel,
         out_shape=(
-            shape(16 * ROWS, LANES), shape(2, 16 * ROWS, LANES), shape(256, LANES), shape(256, LANES),
-            shape(128, LANES), shape(128, LANES),
+            near(16 * ROWS, LANES), near(2, 16 * ROWS, LANES), near(16 * ROWS, LANES), near(1312, LANES),
+            near(800, LANES), shape(256, LANES), shape(256, LANES), shape(128, LANES), shape(128, LANES), shape(400, LANES),
         ),
-        in_specs=[smem(), smem(), smem(), vmem(), vmem(), vmem(), vmem(), anywhere(), anywhere(), anywhere()],
-        out_specs=(vmem(),) * 6,
+        in_specs=[smem()] * 5 + [anywhere()] * 9,
+        out_specs=(vmem(),) * 5 + (anywhere(),) * 5,
         scratch_shapes=[
-            pltpu.VMEM((16 * ROWS, LANES), jnp.float32),
-            pltpu.VMEM((512, LANES), jnp.float32),
-            pltpu.VMEM((16 * PITCH, LANES), jnp.float32),
-            pltpu.VMEM((2, 16 * ROWS, LANES), jnp.float32),
-            pltpu.VMEM((ROWS, LANES), jnp.float32),
-            pltpu.SemaphoreType.DMA((3,)),
+            f32(512, LANES), f32(16 * PITCH, LANES), f32(2, 16 * ROWS, LANES), f32(ROWS, LANES), f32(32, LANES),
+            pltpu.VMEM((256, 128), jnp.bfloat16), pltpu.VMEM((128, 256), jnp.bfloat16),
+            f32(16 * PITCH, LANES), f32(512, LANES), f32(256, LANES), f32(256, LANES), f32(128, LANES), f32(128, LANES),
+            pltpu.SemaphoreType.DMA((14,)),
         ],
         cost_estimate=pl.CostEstimate(flops=500_000_000, bytes_accessed=3_000_000, transcendentals=0),
         name="stiffness",
     )(
-        bucket, blk, band, line, jnp.asarray(twiddle, jnp.float32), jnp.asarray(table, jnp.bfloat16),
-        jnp.asarray(table.T, jnp.bfloat16), fwd, adj, flat(modulus),
+        bucket, radius.reshape(1, NODES), scale, blk, band, jnp.asarray(twiddle, jnp.float32),
+        jnp.asarray(table, jnp.bfloat16), jnp.asarray(table.T, jnp.bfloat16), flat(disp_fwd), flat(disp_adj),
+        flat(modulus), flat(prev_fwd), flat(prev_adj), flat(kernel_in),
     )
-    from_below = shifted(blk_high, "blk", 1)
-    from_above = shifted(blk_low, "blk", -1)
-    band_below = shifted(band_high, "band", 1)
-    band_above = shifted(band_low, "band", -1)
+    far_pairs = [((b, z), (b, z + 1)) for b in range(blks) for z in range(1, bands - 1, 2)]
+    blk_pairs = [((b, z), (b + 1, z)) for b in range(blks - 1) for z in range(bands)]
+    last = lambda pair: pair[0][0] % RUN == RUN - 1
+    even_pairs = [pair for pair in blk_pairs if pair[0][0] % 2 == 0]
+    got_even = swap(even, [pair for pair in even_pairs if (pair[0][0] + 1) % RUN != RUN - 1])
+    got_far = swap(far, [pair for pair in far_pairs if not last(pair)])
+    got_odd = swap(odd, [pair for pair in blk_pairs if pair[0][0] % 2])
+    got_next = swap(even, [pair for pair in even_pairs if (pair[0][0] + 1) % RUN == RUN - 1])
+    got_last = swap(far, [pair for pair in far_pairs if last(pair)])
+    got_chip = swap(chip, [((b, z), (b, z + 1)) for b in range(blks) for z in range(0, bands - 1, 2)])
     base, kernel_out = pl.pallas_call(
         local_kernel,
-        out_shape=(shape(800, LANES), shape(400, LANES)),
-        in_specs=[smem(), smem()] + [vmem()] * 7,
-        out_specs=(vmem(), vmem()),
-        scratch_shapes=[pltpu.VMEM((16 * PITCH, LANES), jnp.float32)],
+        out_shape=(near(800, LANES), shape(400, LANES)),
+        in_specs=[smem(), smem()] + [vmem()] * 5 + [anywhere()],
+        out_specs=(vmem(), anywhere()),
+        scratch_shapes=[f32(16 * PITCH, LANES), f32(512, LANES), pltpu.SemaphoreType.DMA],
+        input_output_aliases={6: 0, 7: 1},
         cost_estimate=pl.CostEstimate(flops=100_000_000, bytes_accessed=3_000_000, transcendentals=0),
         name="local",
-    )(bucket, scale, waves, stiff, fwd, adj, flat(prev_fwd), flat(prev_adj), flat(kernel_in))
+    )(bucket, scale, close(waves), close(stiff), close(field), close(late), close(base), kernel_out)
     next_fwd, next_adj = pl.pallas_call(
         join_kernel,
         out_shape=(shape(400, LANES), shape(400, LANES)),
-        in_specs=[smem()] * 5 + [vmem()] * 5,
+        in_specs=[smem()] * 5 + [vmem()] * 7,
         out_specs=(vmem(), vmem()),
         cost_estimate=pl.CostEstimate(flops=1_000_000, bytes_accessed=1_500_000, transcendentals=0),
         name="join",
     )(
-        bucket, halo_count.reshape(1, 4), blk, band, scale, base, from_below, from_above, band_below, band_above
+        bucket, halo_count.reshape(1, 4), blk, band, scale, close(base), close(got_odd), close(got_even),
+        close(got_chip), close(got_far), close(got_next), close(got_last),
     )
     return tuple(value.reshape(disp_fwd.shape) for value in (next_fwd, next_adj, kernel_out))
 
@@ -430,6 +490,5 @@
     wide = P("blk", "band", None, None)
     line = P("blk", "band", None)
     in_specs = (wide,) * 5 + (line, line, wide, P("blk", "band"), line, wide, wide)
-    return jax.shard_map(
-        per_device, mesh=mesh, in_specs=in_specs, out_specs=(wide, wide, wide), check_vma=False
-    )
+
+    return jax.shard_map(per_device, mesh=mesh, in_specs=in_specs, out_specs=(wide, wide, wide), check_vma=False)

time: 48.6 us -> 41.6 us (0.86)
  Pallas kernels: 14.2 us -> 8.36 us
  local copies, waits for them, and re-layouts: 1.88 us -> 0 us
  starting transfers between devices: 27.1 us -> 27.6 us
    pallas_call x2, Pallas kernels: 12.2 us -> 6.75 us  [the longest x1 5.99 us: per_device(): pl.pallas_call(stiffness_kernel, out_shape=(near(16 * ROWS, LANES), near(...]
    unnamed x10 -> x0, local copies, waits for them, and re-layouts: 1.37 us -> none
    ppermute x4 -> x6, starting transfers between devices: 27.1 us -> 27.6 us  [swap(): return lax.ppermute(value, ('blk', 'band'), pairs)]
    pad x1 -> x0, local copies, waits for them, and re-layouts: 0.51 us -> none  [per_device(): line = jnp.pad(radius.reshape(1, NODES), ((0, 0), (0, LANES - NODES)))]
    ppermute x4 -> x6, waiting for transfers between devices: 3.84 us -> 4 us  [swap(): return lax.ppermute(value, ('blk', 'band'), pairs)]
  transfers between devices with their start and end apart: 4 -> 6, of which waited for: 1 -> 1; matrix products, arithmetic and copies ran while one was open for 0% -> 0% of each run, Pallas kernels for 8% -> 2%
where the time goes in v2:
time: 41.6 us; the launch traced here: 41.3 us
  starting transfers between devices  27.6 us (66%)
  Pallas kernels  8.36 us (20%)
  waiting for transfers between devices  4 us (10%)
  between operations  1.36 us (3%)
    ppermute x6, starting transfers between devices, swap(): return lax.ppermute(value, ('blk', 'band'), pairs)  27.6 us
    pallas_call x1, Pallas kernels, per_device(): pl.pallas_call(stiffness_kernel, out_shape=(near(16 * ROWS, LANES), near(...  5.99 us
    ppermute x6, waiting for transfers between devices, swap(): return lax.ppermute(value, ('blk', 'band'), pairs)  4 us
    pallas_call x1, Pallas kernels, per_device(): pl.pallas_call(join_kernel, out_shape=(shape(400, LANES), shape(400, LANE...  1.61 us
  transfers between devices with their start and end apart: 6, of which 1 were waited for; matrix products, arithmetic and copies ran while one was open for 0% of the time, Pallas kernels for 2%

profile of v2, /device:TPU:7, one launch (start us, length us, event | category | flops | bytes accessed | tf_op | source)
XLA Modules:
  0.0 41.3 jit_solution(14298180130957490136)
XLA Ops:
  1.3 6.0 %stiffness.1 = (f32[896,128]{1,0:T(8,128)S(1)}, f32[2,896,128]{2,1,0:T(8,128)S(1)}, f32[896,128]{1,0:T(8,128)S(1)}, f32[1312,128]{1,0:T(8,128)S(1)}, f32[800,128...) custom-call(s32[1,1]{1,0:T(1,128)S(6)} %copy.28.bucket_ref, ...), custom_call_target="tpu_custom_call" | custom-call | flops 500000000 | bytes 3000000 | tf_op jit(solution)/shard_map/stiffness/pallas_call | solution.py:434
  7.3 2.6 %collective-permute-start.2 = (f32[128,128]{1,0:T(8,128)}, f32[128,128]{1,0:T(8,128)S(1)}, u32[]{:S(2)}, u32[]{:S(2)}) collective-permute-start(f32[128,128]{1,0:T(8,128)} %get-tuple-element.26), channel_id=1, source_target_pairs={{0,1},{1,0},{2,3},{3,2},{4,5},{5,4},{6,7},{7,6},{8,9},{9,8},{10,11... | collective-permute-start | bytes 196616 | tf_op jit(solution)/shard_map/ppermute | solution.py:420
  9.9 16.8 %collective-permute-start = (f32[256,128]{1,0:T(8,128)}, f32[256,128]{1,0:T(8,128)S(1)}, u32[]{:S(2)}, u32[]{:S(2)}) collective-permute-start(f32[256,128]{1,0:T(8,128)} %get-tuple-element.24), channel_id=1, source_target_pairs={{4,8},{5,9},{6,10},{7,11},{8,4},{9,5},{10,6},{11,7},{12,16},{13,17... | collective-permute-start | bytes 393224 | tf_op jit(solution)/shard_map/ppermute | solution.py:420
  26.7 0.7 %collective-permute-start.4 = (f32[256,128]{1,0:T(8,128)}, f32[256,128]{1,0:T(8,128)S(1)}, u32[]{:S(2)}, u32[]{:S(2)}) collective-permute-start(f32[256,128]{1,0:T(8,128)} %get-tuple-element.25), channel_id=1, source_target_pairs={{40,44},{41,45},{42,46},{43,47},{44,40},{45,41},{46,42},{47,43},{8... | collective-permute-start | bytes 393224 | tf_op jit(solution)/shard_map/ppermute | solution.py:420
  27.4 1.9 %collective-permute-start.1 = (f32[256,128]{1,0:T(8,128)}, f32[256,128]{1,0:T(8,128)S(1)}, u32[]{:S(2)}, u32[]{:S(2)}) collective-permute-start(f32[256,128]{1,0:T(8,128)} %get-tuple-element.25), channel_id=1, source_target_pairs={{0,4},{1,5},{2,6},{3,7},{4,0},{5,1},{6,2},{7,3},{8,12},{9,13},{10,... | collective-permute-start | bytes 393224 | tf_op jit(solution)/shard_map/ppermute | solution.py:420
  29.3 0.7 %collective-permute-start.5 = (f32[128,128]{1,0:T(8,128)}, f32[128,128]{1,0:T(8,128)S(1)}, u32[]{:S(2)}, u32[]{:S(2)}) collective-permute-start(f32[128,128]{1,0:T(8,128)} %get-tuple-element.27), channel_id=1, source_target_pairs={{45,46},{46,45},{93,94},{94,93},{141,142},{142,141},{189,190},{190... | collective-permute-start | bytes 196616 | tf_op jit(solution)/shard_map/ppermute | solution.py:420
  30.0 0.0 collective-permute-done.2.chip_ref
  30.0 4.9 %collective-permute-start.3 = (f32[128,128]{1,0:T(8,128)}, f32[128,128]{1,0:T(8,128)S(1)}, u32[]{:S(2)}, u32[]{:S(2)}) collective-permute-start(f32[128,128]{1,0:T(8,128)} %get-tuple-element.27), channel_id=1, source_target_pairs={{1,2},{2,1},{5,6},{6,5},{9,10},{10,9},{13,14},{14,13},{17,18},{18,... | collective-permute-start | bytes 196616 | tf_op jit(solution)/shard_map/ppermute | solution.py:420
  34.9 0.8 %local.1 = (f32[800,128]{1,0:T(8,128)S(1)}, f32[400,128]{1,0:T(8,128)}) custom-call(s32[1,1]{1,0:T(1,128)S(6)} %copy.28.bucket_ref, f32[1,25]{1,0:T(1,128)} %bitcast.16, f32[2,896,128]{2,1,0:T(8,128)S(1)} %get-tuple-element.17.waves_ref, f32[896,128]{1,0:T(8,128)S(1)} %get-tuple-element.18.stiff_ref, ...), custom_call_target="tpu_custom_call", output_to_operand_aliasing={{0}: (6, {}), {1}: (7, {})} | custom-call | flops 100000000 | bytes 3000000 | tf_op jit(solution)/shard_map/local/pallas_call | solution.py:465
  35.7 0.0 collective-permute-done.5.last_ref
  35.7 4.0 %collective-permute-done.3.far_ref = f32[128,128]{1,0:T(8,128)S(1)} collective-permute-done((f32[128,128]{1,0:T(8,128)}, f32[128,128]{1,0:T(8,128)S(1)}, u32[]{:S(2)}, u32[]{:S(2)}) %collective-permute-start.3) | collective-permute-done | bytes 65568 | tf_op jit(solution)/shard_map/ppermute | solution.py:420
  39.7 0.0 collective-permute-done.odd_ref
  39.7 0.0 collective-permute-done.4.next_ref
  39.7 0.0 collective-permute-done.1.even_ref
  39.7 1.6 %join.1 = (f32[400,128]{1,0:T(8,128)}, f32[400,128]{1,0:T(8,128)}) custom-call(s32[1,1]{1,0:T(1,128)S(6)} %copy.28.bucket_ref, s32[1,4]{1,0:T(1,128)} %bitcast.22, s32[2,8]{1,0:T(2,128)} %bitcast.19, s32[2,4]{1,0:T(2,128)} %bitcast.21, f32[1,25]{1,0:T(1,128)} %bitcast.17, f32[800,128]{1,0:T(8,128)S(1)} %get-tuple-element.23.base_ref, ...), custom_call_target="tpu_custom_call" | custom-call | flops 1000000 | bytes 1500000 | tf_op jit(solution)/shard_map/join/pallas_call | solution.py:475
Async XLA Ops:
  7.3 22.7 %collective-permute-start.2 = (f32[128,128]{1,0:T(8,128)}, f32[128,128]{1,0:T(8,128)S(1)}, u32[]{:S(2)}, u32[]{:S(2)}) collective-permute-start(f32[128,128]{1,0:T(8,128)} %get-tuple-element.26), channel_id=1, source_target_pairs={{0,1},{1,0},{2,3},{3,2},{4,5},{5,4},{6,7},{7,6},{8,9},{9,8},{10,11... | collective-permute-start | bytes 196616 | tf_op jit(solution)/shard_map/ppermute | solution.py:420
  9.9 29.8 %collective-permute-start = (f32[256,128]{1,0:T(8,128)}, f32[256,128]{1,0:T(8,128)S(1)}, u32[]{:S(2)}, u32[]{:S(2)}) collective-permute-start(f32[256,128]{1,0:T(8,128)} %get-tuple-element.24), channel_id=1, source_target_pairs={{4,8},{5,9},{6,10},{7,11},{8,4},{9,5},{10,6},{11,7},{12,16},{13,17... | collective-permute-start | bytes 393224 | tf_op jit(solution)/shard_map/ppermute | solution.py:420
  26.7 13.0 %collective-permute-start.4 = (f32[256,128]{1,0:T(8,128)}, f32[256,128]{1,0:T(8,128)S(1)}, u32[]{:S(2)}, u32[]{:S(2)}) collective-permute-start(f32[256,128]{1,0:T(8,128)} %get-tuple-element.25), channel_id=1, source_target_pairs={{40,44},{41,45},{42,46},{43,47},{44,40},{45,41},{46,42},{47,43},{8... | collective-permute-start | bytes 393224 | tf_op jit(solution)/shard_map/ppermute | solution.py:420
  27.4 12.3 %collective-permute-start.1 = (f32[256,128]{1,0:T(8,128)}, f32[256,128]{1,0:T(8,128)S(1)}, u32[]{:S(2)}, u32[]{:S(2)}) collective-permute-start(f32[256,128]{1,0:T(8,128)} %get-tuple-element.25), channel_id=1, source_target_pairs={{0,4},{1,5},{2,6},{3,7},{4,0},{5,1},{6,2},{7,3},{8,12},{9,13},{10,... | collective-permute-start | bytes 393224 | tf_op jit(solution)/shard_map/ppermute | solution.py:420
  29.3 6.4 %collective-permute-start.5 = (f32[128,128]{1,0:T(8,128)}, f32[128,128]{1,0:T(8,128)S(1)}, u32[]{:S(2)}, u32[]{:S(2)}) collective-permute-start(f32[128,128]{1,0:T(8,128)} %get-tuple-element.27), channel_id=1, source_target_pairs={{45,46},{46,45},{93,94},{94,93},{141,142},{142,141},{189,190},{190... | collective-permute-start | bytes 196616 | tf_op jit(solution)/shard_map/ppermute | solution.py:420
  30.0 9.7 %collective-permute-start.3 = (f32[128,128]{1,0:T(8,128)}, f32[128,128]{1,0:T(8,128)S(1)}, u32[]{:S(2)}, u32[]{:S(2)}) collective-permute-start(f32[128,128]{1,0:T(8,128)} %get-tuple-element.27), channel_id=1, source_target_pairs={{1,2},{2,1},{5,6},{6,5},{9,10},{10,9},{13,14},{14,13},{17,18},{18,... | collective-permute-start | bytes 196616 | tf_op jit(solution)/shard_map/ppermute | solution.py:420

commit v3 on v2

v3 whole, which is shorter than its diff:
```python
import math

import jax
import jax.numpy as jnp
import numpy as np
from jax import lax
from jax.experimental import pallas as pl
from jax.experimental.pallas import tpu as pltpu
from jax.sharding import PartitionSpec as P


NODES = 25
ROWS = 56
PITCH = 40
RUN = 12
EARLY_EVEN, EARLY_FAR = 5, 7
LANES = 128


def gll_tables():
    inner_root = math.sqrt(3.0 / 7.0)
    points = np.array([-1.0, -inner_root, 0.0, inner_root, 1.0])
    weights = np.array([0.1, 49.0 / 90.0, 32.0 / 45.0, 49.0 / 90.0, 0.1])
    legendre = (35.0 * points**4 - 30.0 * points**2 + 3.0) / 8.0
    derivative = np.zeros((5, 5))
    for target in range(5):
        for source in range(5):
            if target != source:
                derivative[target, source] = (
                    legendre[target] / legendre[source] / (points[target] - points[source])
                )
    derivative[0, 0] = -5.0
    derivative[4, 4] = 5.0
    return derivative, np.outer(weights, weights)


DERIV, QUAD = gll_tables()


def transform_tables():
    column = np.arange(2 * LANES)
    lane = column % LANES
    sample = 16 * (8 * (column // LANES) + lane % 8) + lane // 8
    angle = 2.0 * np.pi * ((np.arange(256)[:, None] * sample[None, :]) % 256) / 256.0
    table = np.concatenate([np.cos(angle), -np.sin(angle)], axis=0) / 32.0
    turn = (2.0 * np.pi * np.arange(8)[:, None] * column[None, :] / 2048.0).reshape(16, LANES)
    twiddle = np.concatenate([np.cos(turn), np.sin(turn)], axis=0)
    return table, twiddle


def times_root(z, eighth, sign):
    re, im = z
    root = math.sqrt(0.5)
    if eighth == 0:
        return z
    if eighth == 1:
        return ((re - im) * root, (re + im) * root) if sign > 0 else ((re + im) * root, (im - re) * root)
    if eighth == 2:
        return (-im, re) if sign > 0 else (im, -re)
    return ((-re - im) * root, (re - im) * root) if sign > 0 else ((im - re) * root, (-re - im) * root)


def plus(x, y):
    return (x[0] + y[0], x[1] + y[1])


def minus(x, y):
    return (x[0] - y[0], x[1] - y[1])


def plus_turned(x, y, sign):
    return (x[0] - y[1], x[1] + y[0]) if sign > 0 else (x[0] + y[1], x[1] - y[0])


def dft4(a, b, c, d, sign):
    s, t, u, v = plus(a, c), minus(a, c), plus(b, d), minus(b, d)
    return [plus(s, u), plus_turned(t, v, sign), minus(s, u), plus_turned(t, v, -sign)]


def spread(z):
    even = dft4(*z, 1)
    odd = dft4(*(times_root(term, m, 1) for m, term in enumerate(z)), 1)
    return [(even, odd)[k % 2][k // 2] for k in range(8)]


def gathered(v):
    even = dft4(*v[0::2], -1)
    odd = dft4(*v[1::2], -1)
    return [plus(even[m], times_root(odd[m], m, -1)) for m in range(4)]


def centred(table, p):
    e0, o0, e1, o1, c = p[0] + p[4], p[0] - p[4], p[1] + p[3], p[1] - p[3], p[2]
    out = [None] * 5
    for i in range(2):
        t = table[i]
        odd = o0 * float(0.5 * (t[0] - t[4])) + o1 * float(0.5 * (t[1] - t[3]))
        even = e0 * float(0.5 * (t[0] + t[4])) + e1 * float(0.5 * (t[1] + t[3])) + c * float(t[2])
        out[i], out[4 - i] = odd + even, odd - even
    out[2] = o0 * float(table[2, 0]) + o1 * float(table[2, 1])
    return out


def swap_blocks(x):
    lane = lax.broadcasted_iota(jnp.int32, x[0].shape, 1)
    for bit in (4, 2, 1):
        clear = (lane & bit) == 0
        for s in range(8):
            if s & bit:
                continue
            a, b = x[s], x[s | bit]
            x[s] = jnp.where(clear, a, pltpu.roll(b, bit, 1))
            x[s | bit] = jnp.where(clear, pltpu.roll(a, LANES - bit, 1), b)
    return x


def order_limit(bucket):
    return jnp.where(bucket == 0, 16, jnp.where(bucket == 1, 64, jnp.where(bucket == 2, 256, 1024)))


def device_role():
    blk, band = lax.axis_index("blk"), lax.axis_index("band")
    return lax.rem(blk, RUN) == 0, lax.rem(blk, 2), lax.rem(band, 2)


def finish_locally(limit, scale_ref, waves_ref, stiff_ref, field_ref, late_ref, base_ref, slab, kout):
    slot = lax.broadcasted_iota(jnp.int32, (16, LANES), 0)
    order = lax.broadcasted_iota(jnp.int32, (16, LANES), 1) + 128 * (slot % 8)
    kept = order < limit

    def update(n, carry):
        growth = scale_ref[0, n]
        for f in range(2):
            rows = pl.ds(pl.multiple_of(16 * n + 400 * f, 16), 16)
            value = 2.0 * field_ref[rows, :] - late_ref[rows, :] - growth * stiff_ref[rows, :]
            base_ref[rows, :] = jnp.where(kept, value, 0.0)
        return carry

    lax.fori_loop(0, NODES, update, 0, unroll=5)

    for u in range(2):
        p = [
            [[waves_ref[0, u, pl.ds(NODES * f + 5 * i + j, 8, stride=ROWS), :] for j in range(5)] for i in range(5)]
            for f in range(2)
        ]
        total = [
            [
                waves_ref[1, u, pl.ds(5 * i + j, 8, stride=ROWS), :]
                * waves_ref[1, u, pl.ds(NODES + 5 * i + j, 8, stride=ROWS), :]
                for j in range(5)
            ]
            for i in range(5)
        ]
        for i in range(5):
            fwd, adj = centred(DERIV, p[0][i]), centred(DERIV, p[1][i])
            for j in range(5):
                total[i][j] = total[i][j] + fwd[j] * adj[j]
        for j in range(5):
            fwd, adj = (centred(DERIV, [p[f][i][j] for i in range(5)]) for f in range(2))
            for i in range(5):
                slab[u, pl.ds(5 * i + j, 8, stride=PITCH), :] = (total[i][j] + fwd[i] * adj[i]) * float(QUAD[i, j])

    for g in range(4):
        for u in range(2):
            x = swap_blocks([slab[u, pl.ds(PITCH * c + 8 * g, 8), :] for c in range(8)])
            for s in range(8):
                at = 128 * g + 8 * u + s
                kout[pl.ds(at, 8, stride=16), :] = late_ref[pl.ds(800 + at, 8, stride=16), :] - x[s]


SCALARS = (
    pltpu.SMEM((1, 1), jnp.int32), pltpu.SMEM((1, NODES), jnp.float32), pltpu.SMEM((1, NODES), jnp.float32),
    pltpu.SMEM((2, 8), jnp.int32), pltpu.SMEM((2, 4), jnp.int32), pltpu.SMEM((1, 4), jnp.int32),
)


def scalar_loads(sources, targets, sems):
    return [
        pltpu.make_async_copy(source, target, sems.at[i])
        for i, (source, target) in enumerate(zip(sources, targets))
    ]


def stiffness_kernel(
    bucket_hbm, radius_hbm, scale_hbm, blk_hbm, band_hbm, count_hbm, twiddle_hbm, table_hbm, back_hbm, fwd_hbm, adj_hbm, mod_hbm,
    prev_fwd_hbm, prev_adj_hbm, kernel_hbm,
    stiff_ref, waves_ref, field, late, base_ref, odd_hbm, even_hbm, chip_hbm, far_hbm, out_hbm, table_out, growth_out,
    mod, weight, stress, inv, twiddle_ref, table_ref, back_ref, slab, kout, odd_ref, even_ref, chip_ref, far_ref,
    bucket_ref, radius_ref, scale_ref, blk_ref, band_ref, count_ref, sems, scalar_sems,
):
    scalars = scalar_loads(
        (radius_hbm, bucket_hbm, scale_hbm, blk_hbm, band_hbm, count_hbm),
        (radius_ref, bucket_ref, scale_ref, blk_ref, band_ref, count_ref),
        scalar_sems,
    )
    loads = [
        pltpu.make_async_copy(source, target, sems.at[i])
        for i, (source, target) in enumerate((
            (fwd_hbm, field.at[pl.ds(0, 400)]), (adj_hbm, field.at[pl.ds(400, 400)]), (twiddle_hbm, twiddle_ref),
            (table_hbm, table_ref), (mod_hbm, mod.at[pl.ds(0, 400)]), (back_hbm, back_ref),
            (prev_fwd_hbm, late.at[pl.ds(0, 400)]), (prev_adj_hbm, late.at[pl.ds(400, 400)]),
            (kernel_hbm, late.at[pl.ds(800, 400)]),
        ))
    ]
    for load in loads[:2]:
        load.start()
    for load in scalars:
        load.start()
    for load in loads[2:6]:
        load.start()
    for load in scalars:
        load.wait()
    limit = order_limit(bucket_ref[0, 0])
    first, odd, upper = device_role()
    lane8 = lax.broadcasted_iota(jnp.int32, (8, LANES), 1)
    orders = [(lane8 + 128 * a).astype(jnp.float32) for a in range(8)]

    inv[pl.ds(ROWS - 8, 8), :] = jnp.ones((8, LANES), jnp.float32)
    for n in range(NODES):
        line = jnp.full((1, LANES), radius_ref[0, n], jnp.float32)
        inv[pl.ds(n, 1), :] = line
        inv[pl.ds(NODES + n, 1), :] = line
    inv[...] = 1.0 / inv[...]
    for load in loads[:4]:
        load.wait()
    for load in loads[6:]:
        load.start()

    def forward(g, carry):
        inv_r = inv[pl.ds(pl.multiple_of(8 * g, 8), 8), :]
        base = 128 * g
        u, w = [], []
        for a in range(8):
            kept = (lane8 + 128 * a) < limit
            re = jnp.where(kept, field[pl.ds(base + a, 8, stride=16), :], 0.0)
            im = jnp.where(kept, field[pl.ds(base + 8 + a, 8, stride=16), :], 0.0)
            scale = orders[a]
            w.append((-(scale * im) * inv_r, (scale * re) * inv_r))
            u.append((re, im))
        parts = [[], [], [], []]
        for z in (u, w):
            z = [tuple(part.astype(jnp.bfloat16).astype(jnp.float32) for part in term) for term in z]
            for half in range(2):
                for c, (re, im) in enumerate(spread(z[half::2])):
                    if c:
                        at = 2 * c + half
                        cos, sin = twiddle_ref[at : at + 1, :], twiddle_ref[16 + at : 17 + at, :]
                        re, im = re * cos - im * sin, re * sin + im * cos
                    parts[half].append(re)
                    parts[2 + half].append(im)
        lhs = jnp.concatenate([jnp.concatenate(part, axis=0) for part in parts], axis=1)
        out = jnp.dot(lhs.astype(jnp.bfloat16), table_ref[...], preferred_element_type=jnp.float32)
        for t in range(2):
            for c in range(8):
                for half in range(2):
                    at = pl.multiple_of(ROWS * c + 8 * g, 8)
                    waves_ref[t, half, pl.ds(at, 8), :] = out[
                        64 * t + 8 * c : 64 * t + 8 * c + 8, LANES * half : LANES * (half + 1)
                    ]
        return carry

    loads[4].wait()

    def reorder(g, carry):
        for half in range(2):
            x = swap_blocks([mod[pl.ds(128 * g + 8 * half + s, 8, stride=16), :] for s in range(8)])
            for c in range(8):
                weight[half, pl.ds(pl.multiple_of(PITCH * c + 8 * g, 8), 8), :] = x[c]
        return carry

    lax.fori_loop(0, 4, lambda g, carry: reorder(g, forward(g, carry)), 0, unroll=True)
    lax.fori_loop(4, ROWS // 8, forward, 0, unroll=True)

    for u, f in ((0, 0), (0, 1), (1, 0), (1, 1)):
        top = NODES * f
        w = [
            [weight[u, pl.ds(5 * i + j, 8, stride=PITCH), :] * float(QUAD[i, j]) for j in range(5)] for i in range(5)
        ]
        p = [[waves_ref[0, u, pl.ds(top + 5 * i + j, 8, stride=ROWS), :] for j in range(5)] for i in range(5)]
        total = []
        for i in range(5):
            grad = centred(DERIV, p[i])
            total.append(centred(DERIV.T, [w[i][j] * grad[j] for j in range(5)]))
        for j in range(5):
            grad = centred(DERIV, [p[i][j] for i in range(5)])
            part = centred(DERIV.T, [w[i][j] * grad[i] for i in range(5)])
            for i in range(5):
                stress[0, u, pl.ds(top + 5 * i + j, 8, stride=ROWS), :] = total[i][j] + part[i]
        for i in range(5):
            for j in range(5):
                at = pl.ds(top + 5 * i + j, 8, stride=ROWS)
                stress[1, u, at, :] = w[i][j] * waves_ref[1, u, at, :]
    loads[5].wait()

    def backward(g, carry):
        inv_r = inv[pl.ds(pl.multiple_of(8 * g, 8), 8), :]
        at = [pl.ds(pl.multiple_of(ROWS * c + 8 * g, 8), 8) for c in range(8)]
        lhs = jnp.concatenate(
            [
                jnp.concatenate([stress[t, u, at[c], :] for t in range(2) for c in range(8)], axis=0)
                for u in range(2)
            ],
            axis=1,
        )
        out = jnp.dot(lhs.astype(jnp.bfloat16), back_ref[...], preferred_element_type=jnp.float32)
        terms = []
        for t in range(2):
            halves = []
            for half in range(2):
                v = []
                for c in range(8):
                    rows = out[64 * t + 8 * c : 64 * t + 8 * c + 8]
                    re = rows[:, LANES * half : LANES * (half + 1)]
                    im = rows[:, LANES * (2 + half) : LANES * (3 + half)]
                    if c:
                        k = 2 * c + half
                        cos, sin = twiddle_ref[k : k + 1, :], twiddle_ref[16 + k : 17 + k, :]
                        re, im = re * cos + im * sin, im * cos - re * sin
                    v.append((re, im))
                halves.append(gathered(v))
            terms.append([halves[a % 2][a // 2] for a in range(8)])
        for a in range(8):
            kept = (lane8 + 128 * a) < limit
            scale = orders[a]
            re = terms[0][a][0] + (scale * terms[1][a][1]) * inv_r
            im = terms[0][a][1] - (scale * terms[1][a][0]) * inv_r
            stiff_ref[pl.ds(128 * g + a, 8, stride=16), :] = jnp.where(kept, re, 0.0)
            stiff_ref[pl.ds(128 * g + 8 + a, 8, stride=16), :] = jnp.where(kept, im, 0.0)
        return carry

    lax.fori_loop(0, ROWS // 8, backward, 0, unroll=True)

    table_out[0, 0] = limit
    for side in range(2):
        table_out[0, 1 + side] = count_ref[0, side]
        table_out[0, 3 + side] = count_ref[0, 2 + side]
        for k in range(8):
            table_out[0, 8 + 8 * side + k] = blk_ref[side, k]
        for k in range(4):
            table_out[0, 24 + 4 * side + k] = band_ref[side, k]
    for n in range(NODES):
        growth_out[0, n] = scale_ref[0, n]
    sends = []
    for ids, side, slots, ref, hbm in (
        (blk_ref, 1 - odd, 8, even_ref, even_hbm), (blk_ref, odd, 8, odd_ref, odd_hbm),
        (band_ref, upper, 4, far_ref, far_hbm), (band_ref, 1 - upper, 4, chip_ref, chip_hbm),
    ):
        for k in range(slots):
            at = ids[side, k] * 16
            for f in range(2):
                ref[pl.ds((f * slots + k) * 16, 16), :] = stiff_ref[pl.ds(pl.multiple_of(at + 400 * f, 16), 16), :]
        sends.append(pltpu.make_async_copy(ref, hbm, sems.at[10 + len(sends)]))
        sends[-1].start()
    for load in loads[6:]:
        load.wait()

    @pl.when(first)
    def _():
        finish_locally(limit, scale_ref, waves_ref, stiff_ref, field, late, base_ref, slab, kout)
        store = pltpu.make_async_copy(kout.at[pl.ds(0, 400)], out_hbm, sems.at[9])
        store.start()
        store.wait()

    for send in sends:
        send.wait()


def local_kernel(
    numbers_ref, scale_ref, waves_ref, stiff_ref, field_ref, late_ref, base_in, out_in,
    base_ref, out_hbm, slab, kout, sem,
):
    first, _, _ = device_role()

    @pl.when(first)
    def _():
        base_ref[...] = base_in[...]

    @pl.when(jnp.logical_not(first))
    def _():
        limit = numbers_ref[0, 0]
        finish_locally(limit, scale_ref, waves_ref, stiff_ref, field_ref, late_ref, base_ref, slab, kout)
        store = pltpu.make_async_copy(kout.at[pl.ds(0, 400)], out_hbm, sem)
        store.start()
        store.wait()


def join_kernel(
    numbers_ref, scale_ref, base_ref, odd_ref, even_ref, chip_ref, far_ref, next_ref, last_ref,
    fwd_hbm, adj_hbm, total, sems,
):
    _, odd, upper = device_role()
    slot = lax.broadcasted_iota(jnp.int32, (16, LANES), 0)
    order = lax.broadcasted_iota(jnp.int32, (16, LANES), 1) + 128 * (slot % 8)
    kept = order < numbers_ref[0, 0]
    total[...] = base_ref[...]
    stores = []
    for f, out_hbm in enumerate((fwd_hbm, adj_hbm)):
        for start, ids, side, slots, got in (
            (1, 8, odd, 8, (odd_ref,)), (1, 8, 1 - odd, 8, (even_ref, next_ref)),
            (3, 24, 1 - upper, 4, (chip_ref,)), (3, 24, upper, 4, (far_ref, last_ref)),
        ):
            count = numbers_ref[0, start + side]
            for k in range(slots):
                node = numbers_ref[0, ids + slots * side + k]
                take = jnp.logical_and(kept, k < count)
                at = pl.ds(pl.multiple_of(16 * node + 400 * f, 16), 16)
                rows = pl.ds((f * slots + k) * 16, 16)
                step = scale_ref[0, node] * sum(ref[rows, :] for ref in got)
                total[at, :] = base_ref[at, :] - jnp.where(take, step, 0.0)
        stores.append(pltpu.make_async_copy(total.at[pl.ds(400 * f, 400)], out_hbm, sems.at[f]))
        stores[-1].start()
    for store in stores:
        store.wait()


def smem():
    return pl.BlockSpec(memory_space=pltpu.SMEM)


def vmem():
    return pl.BlockSpec(memory_space=pltpu.VMEM)


def anywhere():
    return pl.BlockSpec(memory_space=pl.ANY)


def near(*dims):
    return pltpu.VMEM(dims, jnp.float32)


def shape(*dims):
    return jax.ShapeDtypeStruct(dims, jnp.float32)


def swap(value, chosen):
    bands = lax.axis_size("band")
    pairs = [(b * bands + z, c * bands + y) for (b, z), (c, y) in chosen]
    pairs = sorted(pairs + [(target, source) for source, target in pairs])
    return lax.ppermute(value, ("blk", "band"), pairs)


def per_device(
    disp_fwd, prev_fwd, disp_adj, prev_adj, modulus, radius, step_scale, kernel_in, buckets, halo_count,
    blk_nodes, band_nodes,
):
    flat = lambda value: value.reshape(16 * NODES, LANES)
    inside = lambda value: pltpu.with_memory_space_constraint(value, pltpu.SMEM)
    close = lambda value: pltpu.with_memory_space_constraint(value, pltpu.VMEM)
    table, twiddle = transform_tables()
    bucket, blk, band = buckets.reshape(1, 1), blk_nodes.reshape(2, 8), band_nodes.reshape(2, 4)
    scale = step_scale.reshape(1, NODES)
    blks, bands = lax.axis_size("blk"), lax.axis_size("band")
    f32 = lambda *dims: pltpu.VMEM(dims, jnp.float32)
    stiff, waves, field, late, base, odd, even, chip, far, kernel_out, numbers, growth = pl.pallas_call(
        stiffness_kernel,
        out_shape=(
            near(16 * ROWS, LANES), near(2, 2, 8 * ROWS, LANES), near(16 * ROWS, LANES), near(1312, LANES),
            near(800, LANES), shape(256, LANES), shape(256, LANES), shape(128, LANES), shape(128, LANES), shape(400, LANES),
            pltpu.SMEM((1, 32), jnp.int32), pltpu.SMEM((1, NODES), jnp.float32),
        ),
        in_specs=[anywhere()] * 15,
        out_specs=(vmem(),) * 5 + (anywhere(),) * 5 + (smem(), smem()),
        scratch_shapes=[
            f32(512, LANES), f32(2, 8 * PITCH, LANES), f32(2, 2, 8 * ROWS, LANES), f32(ROWS, LANES), f32(32, LANES),
            pltpu.VMEM((512, 256), jnp.bfloat16), pltpu.VMEM((256, 512), jnp.bfloat16),
            f32(2, 8 * PITCH, LANES), f32(512, LANES), f32(256, LANES), f32(256, LANES), f32(128, LANES), f32(128, LANES),
            *SCALARS, pltpu.SemaphoreType.DMA((14,)), pltpu.SemaphoreType.DMA((6,)),
        ],
        cost_estimate=pl.CostEstimate(flops=500_000_000, bytes_accessed=3_000_000, transcendentals=0),
        name="stiffness",
    )(
        bucket, radius.reshape(1, NODES), scale, blk, band, halo_count.reshape(1, 4), jnp.asarray(twiddle, jnp.float32),
        jnp.asarray(table, jnp.bfloat16), jnp.asarray(table.T, jnp.bfloat16), flat(disp_fwd), flat(disp_adj),
        flat(modulus), flat(prev_fwd), flat(prev_adj), flat(kernel_in),
    )
    far_pairs = [((b, z), (b, z + 1)) for b in range(blks) for z in range(1, bands - 1, 2)]
    blk_pairs = [((b, z), (b + 1, z)) for b in range(blks - 1) for z in range(bands)]
    place = lambda pair: pair[0][0] % RUN
    even_pairs = [pair for pair in blk_pairs if pair[0][0] % 2 == 0]
    got_even = swap(even, [pair for pair in even_pairs if place(pair) < EARLY_EVEN])
    got_far = swap(far, [pair for pair in far_pairs if place(pair) < EARLY_FAR])
    got_odd = swap(odd, [pair for pair in blk_pairs if pair[0][0] % 2])
    got_chip = swap(chip, [((b, z), (b, z + 1)) for b in range(blks) for z in range(0, bands - 1, 2)])
    got_last = swap(far, [pair for pair in far_pairs if place(pair) >= EARLY_FAR])
    got_next = swap(even, [pair for pair in even_pairs if place(pair) >= EARLY_EVEN])
    base, kernel_out = pl.pallas_call(
        local_kernel,
        out_shape=(near(800, LANES), shape(400, LANES)),
        in_specs=[smem()] * 2 + [vmem()] * 5 + [anywhere()],
        out_specs=(vmem(), anywhere()),
        scratch_shapes=[f32(2, 8 * PITCH, LANES), f32(512, LANES), pltpu.SemaphoreType.DMA],
        input_output_aliases={6: 0, 7: 1},
        cost_estimate=pl.CostEstimate(flops=100_000_000, bytes_accessed=3_000_000, transcendentals=0),
        name="local",
    )(inside(numbers), inside(growth), close(waves), close(stiff), close(field), close(late), close(base), kernel_out)
    next_fwd, next_adj = pl.pallas_call(
        join_kernel,
        out_shape=(shape(400, LANES), shape(400, LANES)),
        in_specs=[smem()] * 2 + [vmem()] * 7,
        out_specs=(anywhere(), anywhere()),
        scratch_shapes=[f32(800, LANES), pltpu.SemaphoreType.DMA((2,))],
        cost_estimate=pl.CostEstimate(flops=1_000_000, bytes_accessed=1_500_000, transcendentals=0),
        name="join",
    )(
        inside(numbers), inside(growth), close(base), close(got_odd), close(got_even),
        close(got_chip), close(got_far), close(got_next), close(got_last),
    )
    return tuple(value.reshape(disp_fwd.shape) for value in (next_fwd, next_adj, kernel_out))


def solution(mesh):
    wide = P("blk", "band", None, None)
    line = P("blk", "band", None)
    in_specs = (wide,) * 5 + (line, line, wide, P("blk", "band"), line, wide, wide)

    return jax.shard_map(per_device, mesh=mesh, in_specs=in_specs, out_specs=(wide, wide, wide), check_vma=False)
```

time: 41.6 us -> 40 us (0.962)
  Pallas kernels: 8.36 us -> 6.02 us
  waiting for transfers between devices: 4 us -> 4.66 us
    pallas_call x1, Pallas kernels: 5.99 us -> 5.01 us  [per_device(): pl.pallas_call(stiffness_kernel, out_shape=(near(16 * ROWS, LANES), near(...]
    pallas_call x1, Pallas kernels: 1.61 us -> 0.92 us  [per_device(): pl.pallas_call(join_kernel, out_shape=(shape(400, LANES), shape(400, LANE...]
    ppermute x6, waiting for transfers between devices: 4 us -> 4.66 us  [swap(): return lax.ppermute(value, ('blk', 'band'), pairs)]
    pallas_call x1, Pallas kernels: 0.76 us -> 0.1 us  [per_device(): pl.pallas_call(local_kernel, out_shape=(near(800, LANES), shape(400, LANE...]
  transfers between devices with their start and end apart: 6 -> 6, of which waited for: 1 -> 1; matrix products, arithmetic and copies ran while one was open for 0% -> 0% of each run, Pallas kernels for 2% -> 0%
where the time goes in v3:
time: 40 us; the launch traced here: 39.7 us
  starting transfers between devices  27.7 us (69%)
  Pallas kernels  6.02 us (15%)
  waiting for transfers between devices  4.66 us (12%)
  between operations  1.36 us (3%)
    ppermute x6, starting transfers between devices, swap(): return lax.ppermute(value, ('blk', 'band'), pairs)  27.7 us
    pallas_call x1, Pallas kernels, per_device(): pl.pallas_call(stiffness_kernel, out_shape=(near(16 * ROWS, LANES), near(...  5.01 us
    ppermute x6, waiting for transfers between devices, swap(): return lax.ppermute(value, ('blk', 'band'), pairs)  4.66 us
    pallas_call x1, Pallas kernels, per_device(): pl.pallas_call(join_kernel, out_shape=(shape(400, LANES), shape(400, LANE...  0.92 us
  transfers between devices with their start and end apart: 6, of which 1 were waited for; matrix products, arithmetic and copies ran while one was open for 0% of the time, Pallas kernels for 0%

profile of v3, /device:TPU:7, one launch (start us, length us, event | category | flops | bytes accessed | tf_op | source)
XLA Modules:
  0.0 39.7 jit_solution(6071280136927075149)
XLA Ops:
  1.3 5.0 %stiffness.1 = (f32[896,128]{1,0:T(8,128)S(1)}, f32[2,2,448,128]{3,2,1,0:T(8,128)S(1)}, f32[896,128]{1,0:T(8,128)S(1)}, f32[1312,128]{1,0:T(8,128)S(1)}, f32[800...) custom-call(s32[1,1]{1,0:T(1,128)S(6)} %copy.28.bucket_hbm, ...), custom_call_target="tpu_custom_call" | custom-call | flops 500000000 | bytes 3000000 | tf_op jit(solution)/shard_map/stiffness/pallas_call | solution.py:455
  6.3 2.6 %collective-permute-start.2 = (f32[128,128]{1,0:T(8,128)}, f32[128,128]{1,0:T(8,128)S(1)}, u32[]{:S(2)}, u32[]{:S(2)}) collective-permute-start(f32[128,128]{1,0:T(8,128)} %get-tuple-element.30), channel_id=1, source_target_pairs={{0,1},{1,0},{2,3},{3,2},{4,5},{5,4},{6,7},{7,6},{8,9},{9,8},{10,11... | collective-permute-start | bytes 196616 | tf_op jit(solution)/shard_map/ppermute | solution.py:440
  8.9 16.9 %collective-permute-start = (f32[256,128]{1,0:T(8,128)}, f32[256,128]{1,0:T(8,128)S(1)}, u32[]{:S(2)}, u32[]{:S(2)}) collective-permute-start(f32[256,128]{1,0:T(8,128)} %get-tuple-element.28), channel_id=1, source_target_pairs={{4,8},{5,9},{6,10},{7,11},{8,4},{9,5},{10,6},{11,7},{12,16},{13,17... | collective-permute-start | bytes 393224 | tf_op jit(solution)/shard_map/ppermute | solution.py:440
  25.8 0.7 %collective-permute-start.4 = (f32[256,128]{1,0:T(8,128)}, f32[256,128]{1,0:T(8,128)S(1)}, u32[]{:S(2)}, u32[]{:S(2)}) collective-permute-start(f32[256,128]{1,0:T(8,128)} %get-tuple-element.29), channel_id=1, source_target_pairs={{24,28},{25,29},{26,30},{27,31},{28,24},{29,25},{30,26},{31,27},{3... | collective-permute-start | bytes 393224 | tf_op jit(solution)/shard_map/ppermute | solution.py:440
  26.5 1.9 %collective-permute-start.1 = (f32[256,128]{1,0:T(8,128)}, f32[256,128]{1,0:T(8,128)S(1)}, u32[]{:S(2)}, u32[]{:S(2)}) collective-permute-start(f32[256,128]{1,0:T(8,128)} %get-tuple-element.29), channel_id=1, source_target_pairs={{0,4},{1,5},{2,6},{3,7},{4,0},{5,1},{6,2},{7,3},{8,12},{9,13},{10,... | collective-permute-start | bytes 393224 | tf_op jit(solution)/shard_map/ppermute | solution.py:440
  28.4 0.7 %collective-permute-start.5 = (f32[128,128]{1,0:T(8,128)}, f32[128,128]{1,0:T(8,128)S(1)}, u32[]{:S(2)}, u32[]{:S(2)}) collective-permute-start(f32[128,128]{1,0:T(8,128)} %get-tuple-element.31), channel_id=1, source_target_pairs={{29,30},{30,29},{33,34},{34,33},{37,38},{38,37},{41,42},{42,41},{4... | collective-permute-start | bytes 196616 | tf_op jit(solution)/shard_map/ppermute | solution.py:440
  29.1 0.0 collective-permute-done.2.chip_ref
  29.1 4.9 %collective-permute-start.3 = (f32[128,128]{1,0:T(8,128)}, f32[128,128]{1,0:T(8,128)S(1)}, u32[]{:S(2)}, u32[]{:S(2)}) collective-permute-start(f32[128,128]{1,0:T(8,128)} %get-tuple-element.31), channel_id=1, source_target_pairs={{1,2},{2,1},{5,6},{6,5},{9,10},{10,9},{13,14},{14,13},{17,18},{18,... | collective-permute-start | bytes 196616 | tf_op jit(solution)/shard_map/ppermute | solution.py:440
  34.0 0.1 local.1
  34.1 0.0 collective-permute-done.5.last_ref
  34.1 4.6 %collective-permute-done.3.far_ref = f32[128,128]{1,0:T(8,128)S(1)} collective-permute-done((f32[128,128]{1,0:T(8,128)}, f32[128,128]{1,0:T(8,128)S(1)}, u32[]{:S(2)}, u32[]{:S(2)}) %collective-permute-start.3) | collective-permute-done | bytes 65568 | tf_op jit(solution)/shard_map/ppermute | solution.py:440
  38.8 0.0 collective-permute-done.odd_ref
  38.8 0.0 collective-permute-done.4.next_ref
  38.8 0.0 collective-permute-done.1.even_ref
  38.8 0.9 %join.1 = (f32[400,128]{1,0:T(8,128)}, f32[400,128]{1,0:T(8,128)}) custom-call(s32[1,32]{1,0:T(1,128)S(4)} %get-tuple-element.19.numbers_ref, f32[1,25]{1,0:T(1,128)S(4)} %get-tuple-element.20.scale_ref, f32[800,128]{1,0:T(8,128)S(1)} %get-tuple-element.27.base_ref, f32[256,128]{1,0:T(8,128)S(1)} %collective-permute-done.odd_ref, ...), custom_call_target="tpu_custom_call" | custom-call | flops 1000000 | bytes 1500000 | tf_op jit(solution)/shard_map/join/pallas_call | solution.py:497
Async XLA Ops:
  6.3 22.8 %collective-permute-start.2 = (f32[128,128]{1,0:T(8,128)}, f32[128,128]{1,0:T(8,128)S(1)}, u32[]{:S(2)}, u32[]{:S(2)}) collective-permute-start(f32[128,128]{1,0:T(8,128)} %get-tuple-element.30), channel_id=1, source_target_pairs={{0,1},{1,0},{2,3},{3,2},{4,5},{5,4},{6,7},{7,6},{8,9},{9,8},{10,11... | collective-permute-start | bytes 196616 | tf_op jit(solution)/shard_map/ppermute | solution.py:440
  8.9 29.9 %collective-permute-start = (f32[256,128]{1,0:T(8,128)}, f32[256,128]{1,0:T(8,128)S(1)}, u32[]{:S(2)}, u32[]{:S(2)}) collective-permute-start(f32[256,128]{1,0:T(8,128)} %get-tuple-element.28), channel_id=1, source_target_pairs={{4,8},{5,9},{6,10},{7,11},{8,4},{9,5},{10,6},{11,7},{12,16},{13,17... | collective-permute-start | bytes 393224 | tf_op jit(solution)/shard_map/ppermute | solution.py:440
  25.8 13.0 %collective-permute-start.4 = (f32[256,128]{1,0:T(8,128)}, f32[256,128]{1,0:T(8,128)S(1)}, u32[]{:S(2)}, u32[]{:S(2)}) collective-permute-start(f32[256,128]{1,0:T(8,128)} %get-tuple-element.29), channel_id=1, source_target_pairs={{24,28},{25,29},{26,30},{27,31},{28,24},{29,25},{30,26},{31,27},{3... | collective-permute-start | bytes 393224 | tf_op jit(solution)/shard_map/ppermute | solution.py:440
  26.5 12.3 %collective-permute-start.1 = (f32[256,128]{1,0:T(8,128)}, f32[256,128]{1,0:T(8,128)S(1)}, u32[]{:S(2)}, u32[]{:S(2)}) collective-permute-start(f32[256,128]{1,0:T(8,128)} %get-tuple-element.29), channel_id=1, source_target_pairs={{0,4},{1,5},{2,6},{3,7},{4,0},{5,1},{6,2},{7,3},{8,12},{9,13},{10,... | collective-permute-start | bytes 393224 | tf_op jit(solution)/shard_map/ppermute | solution.py:440
  28.4 5.7 %collective-permute-start.5 = (f32[128,128]{1,0:T(8,128)}, f32[128,128]{1,0:T(8,128)S(1)}, u32[]{:S(2)}, u32[]{:S(2)}) collective-permute-start(f32[128,128]{1,0:T(8,128)} %get-tuple-element.31), channel_id=1, source_target_pairs={{29,30},{30,29},{33,34},{34,33},{37,38},{38,37},{41,42},{42,41},{4... | collective-permute-start | bytes 196616 | tf_op jit(solution)/shard_map/ppermute | solution.py:440
  29.1 9.7 %collective-permute-start.3 = (f32[128,128]{1,0:T(8,128)}, f32[128,128]{1,0:T(8,128)S(1)}, u32[]{:S(2)}, u32[]{:S(2)}) collective-permute-start(f32[128,128]{1,0:T(8,128)} %get-tuple-element.31), channel_id=1, source_target_pairs={{1,2},{2,1},{5,6},{6,5},{9,10},{10,9},{13,14},{14,13},{17,18},{18,... | collective-permute-start | bytes 196616 | tf_op jit(solution)/shard_map/ppermute | solution.py:440

commit v4 on v3

--- a/solution.py
+++ b/solution.py
@@ -196,17 +196,17 @@
     loads = [
         pltpu.make_async_copy(source, target, sems.at[i])
         for i, (source, target) in enumerate((
-            (fwd_hbm, field.at[pl.ds(0, 400)]), (adj_hbm, field.at[pl.ds(400, 400)]), (twiddle_hbm, twiddle_ref),
-            (table_hbm, table_ref), (mod_hbm, mod.at[pl.ds(0, 400)]), (back_hbm, back_ref),
+            (fwd_hbm.at[pl.ds(0, 128)], field.at[pl.ds(0, 128)]), (twiddle_hbm, twiddle_ref), (table_hbm, table_ref),
+            (fwd_hbm.at[pl.ds(128, 272)], field.at[pl.ds(128, 272)]), (adj_hbm, field.at[pl.ds(400, 400)]),
+            (mod_hbm, mod.at[pl.ds(0, 400)]), (back_hbm, back_ref),
             (prev_fwd_hbm, late.at[pl.ds(0, 400)]), (prev_adj_hbm, late.at[pl.ds(400, 400)]),
             (kernel_hbm, late.at[pl.ds(800, 400)]),
         ))
     ]
-    for load in loads[:2]:
-        load.start()
+    loads[0].start()
     for load in scalars:
         load.start()
-    for load in loads[2:6]:
+    for load in loads[1:7]:
         load.start()
     for load in scalars:
         load.wait()
@@ -221,13 +221,11 @@
         inv[pl.ds(n, 1), :] = line
         inv[pl.ds(NODES + n, 1), :] = line
     inv[...] = 1.0 / inv[...]
-    for load in loads[:4]:
+    for load in loads[:2]:
         load.wait()
-    for load in loads[6:]:
-        load.start()
 
     def forward(g, carry):
-        inv_r = inv[pl.ds(pl.multiple_of(8 * g, 8), 8), :]
+        inv_r = inv[pl.ds(8 * g, 8), :]
         base = 128 * g
         u, w = [], []
         for a in range(8):
@@ -249,33 +247,44 @@
                     parts[half].append(re)
                     parts[2 + half].append(im)
         lhs = jnp.concatenate([jnp.concatenate(part, axis=0) for part in parts], axis=1)
+        if g == 0:
+            loads[2].wait()
         out = jnp.dot(lhs.astype(jnp.bfloat16), table_ref[...], preferred_element_type=jnp.float32)
         for t in range(2):
             for c in range(8):
                 for half in range(2):
-                    at = pl.multiple_of(ROWS * c + 8 * g, 8)
+                    at = ROWS * c + 8 * g
                     waves_ref[t, half, pl.ds(at, 8), :] = out[
                         64 * t + 8 * c : 64 * t + 8 * c + 8, LANES * half : LANES * (half + 1)
                     ]
         return carry
 
-    loads[4].wait()
-
     def reorder(g, carry):
         for half in range(2):
             x = swap_blocks([mod[pl.ds(128 * g + 8 * half + s, 8, stride=16), :] for s in range(8)])
             for c in range(8):
-                weight[half, pl.ds(pl.multiple_of(PITCH * c + 8 * g, 8), 8), :] = x[c]
+                weight[half, pl.ds(PITCH * c + 8 * g, 8), :] = x[c]
         return carry
 
-    lax.fori_loop(0, 4, lambda g, carry: reorder(g, forward(g, carry)), 0, unroll=True)
-    lax.fori_loop(4, ROWS // 8, forward, 0, unroll=True)
+    for g in range(ROWS // 8):
+        if g == 1:
+            loads[3].wait()
+        if g == 3:
+            loads[4].wait()
+            loads[5].wait()
+            for load in loads[7:]:
+                load.start()
+        forward(g, 0)
+        if g >= 3:
+            reorder(g - 3, 0)
 
     for u, f in ((0, 0), (0, 1), (1, 0), (1, 1)):
         top = NODES * f
-        w = [
-            [weight[u, pl.ds(5 * i + j, 8, stride=PITCH), :] * float(QUAD[i, j]) for j in range(5)] for i in range(5)
-        ]
+        if f == 0:
+            w = [
+                [weight[u, pl.ds(5 * i + j, 8, stride=PITCH), :] * float(QUAD[i, j]) for j in range(5)]
+                for i in range(5)
+            ]
         p = [[waves_ref[0, u, pl.ds(top + 5 * i + j, 8, stride=ROWS), :] for j in range(5)] for i in range(5)]
         total = []
         for i in range(5):
@@ -290,11 +299,11 @@
             for j in range(5):
                 at = pl.ds(top + 5 * i + j, 8, stride=ROWS)
                 stress[1, u, at, :] = w[i][j] * waves_ref[1, u, at, :]
-    loads[5].wait()
+    loads[6].wait()
 
     def backward(g, carry):
-        inv_r = inv[pl.ds(pl.multiple_of(8 * g, 8), 8), :]
-        at = [pl.ds(pl.multiple_of(ROWS * c + 8 * g, 8), 8) for c in range(8)]
+        inv_r = inv[pl.ds(8 * g, 8), :]
+        at = [pl.ds(ROWS * c + 8 * g, 8) for c in range(8)]
         lhs = jnp.concatenate(
             [
                 jnp.concatenate([stress[t, u, at[c], :] for t in range(2) for c in range(8)], axis=0)
@@ -328,7 +337,8 @@
             stiff_ref[pl.ds(128 * g + 8 + a, 8, stride=16), :] = jnp.where(kept, im, 0.0)
         return carry
 
-    lax.fori_loop(0, ROWS // 8, backward, 0, unroll=True)
+    for g in range(ROWS // 8):
+        backward(g, 0)
 
     table_out[0, 0] = limit
     for side in range(2):
@@ -349,15 +359,15 @@
             at = ids[side, k] * 16
             for f in range(2):
                 ref[pl.ds((f * slots + k) * 16, 16), :] = stiff_ref[pl.ds(pl.multiple_of(at + 400 * f, 16), 16), :]
-        sends.append(pltpu.make_async_copy(ref, hbm, sems.at[10 + len(sends)]))
+        sends.append(pltpu.make_async_copy(ref, hbm, sems.at[11 + len(sends)]))
         sends[-1].start()
-    for load in loads[6:]:
+    for load in loads[7:]:
         load.wait()
 
     @pl.when(first)
     def _():
         finish_locally(limit, scale_ref, waves_ref, stiff_ref, field, late, base_ref, slab, kout)
-        store = pltpu.make_async_copy(kout.at[pl.ds(0, 400)], out_hbm, sems.at[9])
+        store = pltpu.make_async_copy(kout.at[pl.ds(0, 400)], out_hbm, sems.at[10])
         store.start()
         store.wait()
 
@@ -465,7 +475,7 @@
             f32(512, LANES), f32(2, 8 * PITCH, LANES), f32(2, 2, 8 * ROWS, LANES), f32(ROWS, LANES), f32(32, LANES),
             pltpu.VMEM((512, 256), jnp.bfloat16), pltpu.VMEM((256, 512), jnp.bfloat16),
             f32(2, 8 * PITCH, LANES), f32(512, LANES), f32(256, LANES), f32(256, LANES), f32(128, LANES), f32(128, LANES),
-            *SCALARS, pltpu.SemaphoreType.DMA((14,)), pltpu.SemaphoreType.DMA((6,)),
+            *SCALARS, pltpu.SemaphoreType.DMA((15,)), pltpu.SemaphoreType.DMA((6,)),
         ],
         cost_estimate=pl.CostEstimate(flops=500_000_000, bytes_accessed=3_000_000, transcendentals=0),
         name="stiffness",

time: 40 us -> 40 us (level)
  no operation moved by 1% of the time
where the time goes in v4:
time: 40 us; the launch traced here: 39.7 us
  starting transfers between devices  27.7 us (69%)
  Pallas kernels  6.05 us (15%)
  waiting for transfers between devices  4.66 us (12%)
  between operations  1.36 us (3%)
    ppermute x6, starting transfers between devices, swap(): return lax.ppermute(value, ('blk', 'band'), pairs)  27.7 us
    pallas_call x1, Pallas kernels, per_device(): pl.pallas_call(stiffness_kernel, out_shape=(near(16 * ROWS, LANES), near(...  5.03 us
    ppermute x6, waiting for transfers between devices, swap(): return lax.ppermute(value, ('blk', 'band'), pairs)  4.66 us
    pallas_call x1, Pallas kernels, per_device(): pl.pallas_call(join_kernel, out_shape=(shape(400, LANES), shape(400, LANE...  0.92 us
  transfers between devices with their start and end apart: 6, of which 1 were waited for; matrix products, arithmetic and copies ran while one was open for 0% of the time, Pallas kernels for 0%

profile of v4, /device:TPU:7, one launch (start us, length us, event | category | flops | bytes accessed | tf_op | source)
XLA Modules:
  0.0 39.7 jit_solution(14702232656579414282)
XLA Ops:
  1.3 5.0 %stiffness.1 = (f32[896,128]{1,0:T(8,128)S(1)}, f32[2,2,448,128]{3,2,1,0:T(8,128)S(1)}, f32[896,128]{1,0:T(8,128)S(1)}, f32[1312,128]{1,0:T(8,128)S(1)}, f32[800...) custom-call(s32[1,1]{1,0:T(1,128)S(6)} %copy.28.bucket_hbm, ...), custom_call_target="tpu_custom_call" | custom-call | flops 500000000 | bytes 3000000 | tf_op jit(solution)/shard_map/stiffness/pallas_call | solution.py:465
  6.3 2.6 %collective-permute-start.2 = (f32[128,128]{1,0:T(8,128)}, f32[128,128]{1,0:T(8,128)S(1)}, u32[]{:S(2)}, u32[]{:S(2)}) collective-permute-start(f32[128,128]{1,0:T(8,128)} %get-tuple-element.30), channel_id=1, source_target_pairs={{0,1},{1,0},{2,3},{3,2},{4,5},{5,4},{6,7},{7,6},{8,9},{9,8},{10,11... | collective-permute-start | bytes 196616 | tf_op jit(solution)/shard_map/ppermute | solution.py:450
  8.9 16.9 %collective-permute-start = (f32[256,128]{1,0:T(8,128)}, f32[256,128]{1,0:T(8,128)S(1)}, u32[]{:S(2)}, u32[]{:S(2)}) collective-permute-start(f32[256,128]{1,0:T(8,128)} %get-tuple-element.28), channel_id=1, source_target_pairs={{4,8},{5,9},{6,10},{7,11},{8,4},{9,5},{10,6},{11,7},{12,16},{13,17... | collective-permute-start | bytes 393224 | tf_op jit(solution)/shard_map/ppermute | solution.py:450
  25.8 0.7 %collective-permute-start.4 = (f32[256,128]{1,0:T(8,128)}, f32[256,128]{1,0:T(8,128)S(1)}, u32[]{:S(2)}, u32[]{:S(2)}) collective-permute-start(f32[256,128]{1,0:T(8,128)} %get-tuple-element.29), channel_id=1, source_target_pairs={{24,28},{25,29},{26,30},{27,31},{28,24},{29,25},{30,26},{31,27},{3... | collective-permute-start | bytes 393224 | tf_op jit(solution)/shard_map/ppermute | solution.py:450
  26.5 1.9 %collective-permute-start.1 = (f32[256,128]{1,0:T(8,128)}, f32[256,128]{1,0:T(8,128)S(1)}, u32[]{:S(2)}, u32[]{:S(2)}) collective-permute-start(f32[256,128]{1,0:T(8,128)} %get-tuple-element.29), channel_id=1, source_target_pairs={{0,4},{1,5},{2,6},{3,7},{4,0},{5,1},{6,2},{7,3},{8,12},{9,13},{10,... | collective-permute-start | bytes 393224 | tf_op jit(solution)/shard_map/ppermute | solution.py:450
  28.4 0.7 %collective-permute-start.5 = (f32[128,128]{1,0:T(8,128)}, f32[128,128]{1,0:T(8,128)S(1)}, u32[]{:S(2)}, u32[]{:S(2)}) collective-permute-start(f32[128,128]{1,0:T(8,128)} %get-tuple-element.31), channel_id=1, source_target_pairs={{29,30},{30,29},{33,34},{34,33},{37,38},{38,37},{41,42},{42,41},{4... | collective-permute-start | bytes 196616 | tf_op jit(solution)/shard_map/ppermute | solution.py:450
  29.1 0.0 collective-permute-done.2.chip_ref
  29.1 4.9 %collective-permute-start.3 = (f32[128,128]{1,0:T(8,128)}, f32[128,128]{1,0:T(8,128)S(1)}, u32[]{:S(2)}, u32[]{:S(2)}) collective-permute-start(f32[128,128]{1,0:T(8,128)} %get-tuple-element.31), channel_id=1, source_target_pairs={{1,2},{2,1},{5,6},{6,5},{9,10},{10,9},{13,14},{14,13},{17,18},{18,... | collective-permute-start | bytes 196616 | tf_op jit(solution)/shard_map/ppermute | solution.py:450
  34.0 0.1 local.1
  34.2 0.0 collective-permute-done.5.last_ref
  34.2 4.6 %collective-permute-done.3.far_ref = f32[128,128]{1,0:T(8,128)S(1)} collective-permute-done((f32[128,128]{1,0:T(8,128)}, f32[128,128]{1,0:T(8,128)S(1)}, u32[]{:S(2)}, u32[]{:S(2)}) %collective-permute-start.3) | collective-permute-done | bytes 65568 | tf_op jit(solution)/shard_map/ppermute | solution.py:450
  38.8 0.0 collective-permute-done.odd_ref
  38.8 0.0 collective-permute-done.4.next_ref
  38.8 0.0 collective-permute-done.1.even_ref
  38.8 0.9 %join.1 = (f32[400,128]{1,0:T(8,128)}, f32[400,128]{1,0:T(8,128)}) custom-call(s32[1,32]{1,0:T(1,128)S(4)} %get-tuple-element.19.numbers_ref, f32[1,25]{1,0:T(1,128)S(4)} %get-tuple-element.20.scale_ref, f32[800,128]{1,0:T(8,128)S(1)} %get-tuple-element.27.base_ref, f32[256,128]{1,0:T(8,128)S(1)} %collective-permute-done.odd_ref, ...), custom_call_target="tpu_custom_call" | custom-call | flops 1000000 | bytes 1500000 | tf_op jit(solution)/shard_map/join/pallas_call | solution.py:507
Async XLA Ops:
  6.3 22.8 %collective-permute-start.2 = (f32[128,128]{1,0:T(8,128)}, f32[128,128]{1,0:T(8,128)S(1)}, u32[]{:S(2)}, u32[]{:S(2)}) collective-permute-start(f32[128,128]{1,0:T(8,128)} %get-tuple-element.30), channel_id=1, source_target_pairs={{0,1},{1,0},{2,3},{3,2},{4,5},{5,4},{6,7},{7,6},{8,9},{9,8},{10,11... | collective-permute-start | bytes 196616 | tf_op jit(solution)/shard_map/ppermute | solution.py:450
  8.9 29.9 %collective-permute-start = (f32[256,128]{1,0:T(8,128)}, f32[256,128]{1,0:T(8,128)S(1)}, u32[]{:S(2)}, u32[]{:S(2)}) collective-permute-start(f32[256,128]{1,0:T(8,128)} %get-tuple-element.28), channel_id=1, source_target_pairs={{4,8},{5,9},{6,10},{7,11},{8,4},{9,5},{10,6},{11,7},{12,16},{13,17... | collective-permute-start | bytes 393224 | tf_op jit(solution)/shard_map/ppermute | solution.py:450
  25.8 13.0 %collective-permute-start.4 = (f32[256,128]{1,0:T(8,128)}, f32[256,128]{1,0:T(8,128)S(1)}, u32[]{:S(2)}, u32[]{:S(2)}) collective-permute-start(f32[256,128]{1,0:T(8,128)} %get-tuple-element.29), channel_id=1, source_target_pairs={{24,28},{25,29},{26,30},{27,31},{28,24},{29,25},{30,26},{31,27},{3... | collective-permute-start | bytes 393224 | tf_op jit(solution)/shard_map/ppermute | solution.py:450
  26.5 12.3 %collective-permute-start.1 = (f32[256,128]{1,0:T(8,128)}, f32[256,128]{1,0:T(8,128)S(1)}, u32[]{:S(2)}, u32[]{:S(2)}) collective-permute-start(f32[256,128]{1,0:T(8,128)} %get-tuple-element.29), channel_id=1, source_target_pairs={{0,4},{1,5},{2,6},{3,7},{4,0},{5,1},{6,2},{7,3},{8,12},{9,13},{10,... | collective-permute-start | bytes 393224 | tf_op jit(solution)/shard_map/ppermute | solution.py:450
  28.4 5.7 %collective-permute-start.5 = (f32[128,128]{1,0:T(8,128)}, f32[128,128]{1,0:T(8,128)S(1)}, u32[]{:S(2)}, u32[]{:S(2)}) collective-permute-start(f32[128,128]{1,0:T(8,128)} %get-tuple-element.31), channel_id=1, source_target_pairs={{29,30},{30,29},{33,34},{34,33},{37,38},{38,37},{41,42},{42,41},{4... | collective-permute-start | bytes 196616 | tf_op jit(solution)/shard_map/ppermute | solution.py:450
  29.1 9.7 %collective-permute-start.3 = (f32[128,128]{1,0:T(8,128)}, f32[128,128]{1,0:T(8,128)S(1)}, u32[]{:S(2)}, u32[]{:S(2)}) collective-permute-start(f32[128,128]{1,0:T(8,128)} %get-tuple-element.31), channel_id=1, source_target_pairs={{1,2},{2,1},{5,6},{6,5},{9,10},{10,9},{13,14},{14,13},{17,18},{18,... | collective-permute-start | bytes 196616 | tf_op jit(solution)/shard_map/ppermute | solution.py:450
